TPU v7x, 32 devices: a whole 2x2x4 slice. The times are simulated.
32 devices in a mesh: dp: 4 (over x, y), ep: 8 (over z, core).
Axes of the slice: x: 2, y: 2, z: 4, core: 2. Of those that a mesh axis runs over, the one named last changes fastest.
Arguments:
- x_a: bfloat16 [32768, 768], P(('dp', 'ep')), parts along dimension 0
- x_b: bfloat16 [32768, 768], P(('dp', 'ep')), parts along dimension 0
- dy_b: bfloat16 [32768, 768], P(('dp', 'ep')), parts along dimension 0
- w_q: bfloat16 [768, 768], replicated
- w_k: bfloat16 [768, 768], replicated
- w_v: bfloat16 [768, 768], replicated
- w_o: bfloat16 [768, 768], replicated
- gain_attn: float32 [768], replicated
- gain_moe: float32 [768], replicated
- w_gate: bfloat16 [8, 768, 3072], P('ep')
- w_up: bfloat16 [8, 768, 3072], P('ep')
- w_down: bfloat16 [8, 3072, 768], P('ep')
- expert_a: int32 [32768, 1], P(('dp', 'ep')), parts along dimension 0
- slot_a: int32 [32768, 1], P(('dp', 'ep')), parts along dimension 0
- gate_a: bfloat16 [32768, 1], P(('dp', 'ep')), parts along dimension 0
- expert_b: int32 [32768, 1], P(('dp', 'ep')), parts along dimension 0
- slot_b: int32 [32768, 1], P(('dp', 'ep')), parts along dimension 0
- gate_b: bfloat16 [32768, 1], P(('dp', 'ep')), parts along dimension 0
Outputs:
- output 1: bfloat16 [32768, 768], P(('dp', 'ep')), parts along dimension 0
- output 2: bfloat16 [32768, 768], P(('dp', 'ep')), parts along dimension 0
- output 3: float32 [3072, 768], P('dp'), parts along dimension 0
- output 4: float32 [3072, 768], P('dp'), parts along dimension 0
- output 5: float32 [3072, 768], P('dp'), parts along dimension 0
- output 6: float32 [3072, 768], P('dp'), parts along dimension 0
- output 7: float32 [32, 768, 3072], P(('dp', 'ep')), parts along dimension 0
- output 8: float32 [32, 768, 3072], P(('dp', 'ep')), parts along dimension 0
- output 9: float32 [32, 3072, 768], P(('dp', 'ep')), parts along dimension 0
There are 4 independent parts. A program takes and returns all parts, laid end to end along the dimension named above; an argument that names none is the same for every part.
All inputs are finite; a program needn't handle non-finite values.
Results may differ from a plain program's by a relative error of at most 0.0168784.
Values are sent between devices in bfloat16 or wider.
A program may use at most 1 GiB of HBM per device.

v0:
```python
import jax
import jax.numpy as jnp
from jax import lax
from jax.sharding import PartitionSpec as P

RMS_EPS = 1e-6
HEAD_DIM = 128
SEQ_MAX = 256


def capacity_of(tokens, choices, num_experts):
    return ((3 * tokens * choices // num_experts + 7) // 8) * 8


def rms_norm(row_block, gain_vec):
    rows_f = row_block.astype(jnp.float32)
    inv_rms = lax.rsqrt(jnp.mean(rows_f * rows_f, axis=-1, keepdims=True) + RMS_EPS)
    return (rows_f * inv_rms * gain_vec).astype(jnp.bfloat16)


def attn_forward(x_rows, w_q, w_k, w_v, w_o, gain_attn):
    tokens, hidden = x_rows.shape
    seq_len = min(tokens, SEQ_MAX)
    head_shape = (tokens // seq_len, seq_len, hidden // HEAD_DIM, HEAD_DIM)
    normed, norm_vjp = jax.vjp(lambda rows_in: rms_norm(rows_in, gain_attn), x_rows)

    def project(weight):
        return jnp.dot(normed, weight, preferred_element_type=jnp.float32).astype(jnp.bfloat16).reshape(head_shape)

    q_heads = project(w_q)
    k_heads = project(w_k)
    v_heads = project(w_v)
    scores = jnp.einsum('bqhd,bkhd->bhqk', q_heads, k_heads, preferred_element_type=jnp.float32) * HEAD_DIM ** -0.5
    causal = jnp.arange(seq_len)[:, None] >= jnp.arange(seq_len)[None, :]
    attn_probs = jax.nn.softmax(jnp.where(causal, scores, -1e30), axis=-1)
    probs_low = attn_probs.astype(jnp.bfloat16)
    mixed_rows = jnp.einsum('bhqk,bkhd->bqhd', probs_low, v_heads, preferred_element_type=jnp.float32).astype(jnp.bfloat16).reshape(tokens, hidden)
    h_rows = (x_rows.astype(jnp.float32) + jnp.dot(mixed_rows, w_o, preferred_element_type=jnp.float32)).astype(jnp.bfloat16)
    return h_rows, (normed, norm_vjp, q_heads, k_heads, v_heads, attn_probs, probs_low, mixed_rows)


def attn_backward(d_h, saved, w_q, w_k, w_v, w_o):
    normed, norm_vjp, q_heads, k_heads, v_heads, attn_probs, probs_low, mixed_rows = saved
    tokens, hidden = mixed_rows.shape
    d_wo = jnp.einsum('td,te->de', mixed_rows, d_h, preferred_element_type=jnp.float32)
    d_mixed = jnp.einsum('te,de->td', d_h, w_o, preferred_element_type=jnp.float32).astype(jnp.bfloat16).reshape(q_heads.shape)
    d_probs = jnp.einsum('bqhd,bkhd->bhqk', d_mixed, v_heads, preferred_element_type=jnp.float32)
    d_v = jnp.einsum('bhqk,bqhd->bkhd', probs_low, d_mixed, preferred_element_type=jnp.float32).astype(jnp.bfloat16).reshape(tokens, hidden)
    d_scores = (attn_probs * (d_probs - jnp.sum(d_probs * attn_probs, axis=-1, keepdims=True)) * HEAD_DIM ** -0.5).astype(jnp.bfloat16)
    d_q = jnp.einsum('bhqk,bkhd->bqhd', d_scores, k_heads, preferred_element_type=jnp.float32).astype(jnp.bfloat16).reshape(tokens, hidden)
    d_k = jnp.einsum('bhqk,bqhd->bkhd', d_scores, q_heads, preferred_element_type=jnp.float32).astype(jnp.bfloat16).reshape(tokens, hidden)
    d_wq = jnp.einsum('td,te->de', normed, d_q, preferred_element_type=jnp.float32)
    d_wk = jnp.einsum('td,te->de', normed, d_k, preferred_element_type=jnp.float32)
    d_wv = jnp.einsum('td,te->de', normed, d_v, preferred_element_type=jnp.float32)
    d_normed = (jnp.einsum('te,de->td', d_q, w_q, preferred_element_type=jnp.float32) + jnp.einsum('te,de->td', d_k, w_k, preferred_element_type=jnp.float32) + jnp.einsum('te,de->td', d_v, w_v, preferred_element_type=jnp.float32)).astype(jnp.bfloat16)
    d_x = (d_h.astype(jnp.float32) + norm_vjp(d_normed)[0].astype(jnp.float32)).astype(jnp.bfloat16)
    return d_x, jnp.stack([d_wq, d_wk, d_wv, d_wo])


def routing_tables(expert_ids, slot_ids, gate_vals, num_experts, slot_count):
    tokens, choices = expert_ids.shape
    sentinel = num_experts * slot_count
    flat_pos = jnp.where(slot_ids >= 0, expert_ids * slot_count + slot_ids, sentinel)
    token_of = jnp.broadcast_to(jnp.arange(tokens, dtype=jnp.int32)[:, None], (tokens, choices))
    inv_tok = jnp.full((sentinel + 1,), tokens, jnp.int32).at[flat_pos.reshape(-1)].set(token_of.reshape(-1))[:sentinel]
    inv_gate = jnp.zeros((sentinel + 1,), jnp.bfloat16).at[flat_pos.reshape(-1)].set(gate_vals.reshape(-1))[:sentinel]
    return flat_pos, inv_tok, inv_gate


def with_zero_row(row_block):
    return jnp.concatenate([row_block, jnp.zeros((1, row_block.shape[1]), row_block.dtype)], axis=0)


def dispatch(row_block, inv_tok, num_experts, slot_count):
    return jnp.take(with_zero_row(row_block), inv_tok, axis=0).reshape(num_experts, slot_count, row_block.shape[1])


def gather_choices(back_rows, flat_pos):
    return jnp.take(with_zero_row(back_rows.reshape(-1, back_rows.shape[-1])), flat_pos, axis=0)


def combine(h_rows, back_rows, flat_pos, gate_vals):
    mix_sum = jnp.einsum('tk,tkd->td', gate_vals, gather_choices(back_rows, flat_pos), preferred_element_type=jnp.float32)
    return (h_rows.astype(jnp.float32) + mix_sum).astype(jnp.bfloat16)


def expert_hidden(expert_in, w_gate, w_up):
    z_gate = jnp.einsum('ecd,edf->ecf', expert_in, w_gate, preferred_element_type=jnp.float32)
    z_up = jnp.einsum('ecd,edf->ecf', expert_in, w_up, preferred_element_type=jnp.float32)
    return z_gate, z_up, (jax.nn.silu(z_gate) * z_up).astype(jnp.bfloat16)


def expert_output(hidden_act, w_down):
    return jnp.einsum('ecf,efd->ecd', hidden_act, w_down, preferred_element_type=jnp.float32).astype(jnp.bfloat16)


def expert_backward(d_out, expert_in, z_gate, z_up, hidden_act, w_gate, w_up, w_down):
    d_wdown = jnp.einsum('ecf,ecd->efd', hidden_act, d_out, preferred_element_type=jnp.float32)
    d_act = jnp.einsum('ecd,efd->ecf', d_out, w_down, preferred_element_type=jnp.float32).astype(jnp.bfloat16)
    sigmoid_g = jax.nn.sigmoid(z_gate)
    d_zgate = (d_act * z_up * sigmoid_g * (1.0 + z_gate * (1.0 - sigmoid_g))).astype(jnp.bfloat16)
    d_zup = (d_act * z_gate * sigmoid_g).astype(jnp.bfloat16)
    d_wgate = jnp.einsum('ecd,ecf->edf', expert_in, d_zgate, preferred_element_type=jnp.float32)
    d_wup = jnp.einsum('ecd,ecf->edf', expert_in, d_zup, preferred_element_type=jnp.float32)
    d_in = (jnp.einsum('ecf,edf->ecd', d_zgate, w_gate, preferred_element_type=jnp.float32) + jnp.einsum('ecf,edf->ecd', d_zup, w_up, preferred_element_type=jnp.float32)).astype(jnp.bfloat16)
    return d_in, d_wgate, d_wup, d_wdown


def solution(mesh):
    group_size = mesh.shape['ep']
    row_spec = P(('dp', 'ep'), None)
    rep_two = P(None, None)
    rep_one = P(None)
    expert_spec = P('ep', None, None)
    grad_spec = P('dp', None)
    expert_grad_spec = P(('dp', 'ep'), None, None)

    def device_program(x_a, x_b, dy_b, w_q, w_k, w_v, w_o, gain_attn, gain_moe, w_gate, w_up, w_down, expert_a, slot_a, gate_a, expert_b, slot_b, gate_b):
        tokens = x_a.shape[0]
        num_experts = w_gate.shape[0] * group_size
        slot_count = capacity_of(tokens, expert_a.shape[1], num_experts)

        h_a, _ = attn_forward(x_a, w_q, w_k, w_v, w_o, gain_attn)
        u_a = rms_norm(h_a, gain_moe)
        pos_a, inv_tok_a, _ = routing_tables(expert_a, slot_a, gate_a, num_experts, slot_count)
        recv_a = lax.all_to_all(dispatch(u_a, inv_tok_a, num_experts, slot_count), 'ep', 0, 1, tiled=True)
        _, _, act_a = expert_hidden(recv_a, w_gate, w_up)
        back_a = lax.all_to_all(expert_output(act_a, w_down), 'ep', 1, 0, tiled=True)
        y_a = combine(h_a, back_a, pos_a, gate_a)

        h_b, saved_b = attn_forward(x_b, w_q, w_k, w_v, w_o, gain_attn)
        u_b, norm_vjp_b = jax.vjp(lambda rows_in: rms_norm(rows_in, gain_moe), h_b)
        pos_b, inv_tok_b, inv_gate_b = routing_tables(expert_b, slot_b, gate_b, num_experts, slot_count)
        recv_b = lax.all_to_all(dispatch(u_b, inv_tok_b, num_experts, slot_count), 'ep', 0, 1, tiled=True)
        z_gate_b, z_up_b, act_b = expert_hidden(recv_b, w_gate, w_up)
        d_send = (jnp.take(with_zero_row(dy_b), inv_tok_b, axis=0) * inv_gate_b[:, None]).reshape(num_experts, slot_count, -1)
        d_out_b = lax.all_to_all(d_send, 'ep', 0, 1, tiled=True)
        d_in_b, d_wgate, d_wup, d_wdown = expert_backward(d_out_b, recv_b, z_gate_b, z_up_b, act_b, w_gate, w_up, w_down)
        d_back = lax.all_to_all(d_in_b, 'ep', 1, 0, tiled=True)
        d_u = jnp.sum(gather_choices(d_back, pos_b), axis=1, dtype=jnp.float32).astype(jnp.bfloat16)
        d_h = (dy_b.astype(jnp.float32) + norm_vjp_b(d_u)[0].astype(jnp.float32)).astype(jnp.bfloat16)
        d_x, attn_grads = attn_backward(d_h, saved_b, w_q, w_k, w_v, w_o)
        attn_grads = lax.psum(attn_grads, 'ep')
        return (y_a, d_x, attn_grads[0], attn_grads[1], attn_grads[2], attn_grads[3], d_wgate, d_wup, d_wdown)

    return jax.shard_map(device_program, mesh=mesh, in_specs=(row_spec, row_spec, row_spec, rep_two, rep_two, rep_two, rep_two, rep_one, rep_one, expert_spec, expert_spec, expert_spec, row_spec, row_spec, row_spec, row_spec, row_spec, row_spec), out_specs=(row_spec, row_spec, grad_spec, grad_spec, grad_spec, grad_spec, expert_grad_spec, expert_grad_spec, expert_grad_spec), check_vma=False)
```

profile of v0, /device:TPU:0, one launch (start us, length us, event | category | flops | bytes accessed | tf_op | source)
XLA Modules:
  0.0 1310.3 jit_solution(18073601638257953780)
XLA Ops:
  76.0 13.6 %gather_fusion.2 = bf16[3072,768]{1,0:T(8,128)(2,1)} fusion(bf16[1025,768]{1,0:T(8,128)(2,1)S(1)} %concatenate.17, s32[3072]{0:T(1024)S(1)} %fusion.107), kind=kCustom, calls=%fused_computation.2.clone | custom fusion | bytes 9449472 | tf_op jit(solution)/shard_map/jit(_take)/gather | solution.py:136
  89.6 16.2 %gather_fusion.3 = bf16[3072,768]{1,0:T(8,128)(2,1)} fusion(bf16[1025,768]{1,0:T(8,128)(2,1)} %concatenate.18, s32[3072]{0:T(1024)S(1)} %fusion.107), kind=kCustom, calls=%fused_computation.3.clone | custom fusion | bytes 9449472 | tf_op jit(solution)/shard_map/jit(_take)/gather | solution.py:75
  112.7 111.4 %all_to_all.20 = bf16[8,384,768]{2,1,0:T(8,128)(2,1)} all-to-all(bf16[8,384,768]{2,1,0:T(8,128)(2,1)S(1)} %bitcast.185), channel_id=1, replica_groups=mesh['dp'=4,'ep'=8] {'ep'}, dimensions={0} | all-to-all | bytes 9437184 | tf_op jit(solution)/shard_map/all_to_all | solution.py:137
  229.0 20.9 %convolution_convert_fusion = bf16[3072,3072]{1,0:T(8,128)(2,1)} fusion(bf16[3072,768]{1,0:T(8,128)(2,1)} %bitcast.193, bf16[1,3072,768]{2,1,0:T(8,128)(2,1)} %param.33), kind=kOutput, calls=%fused_computation.22 | convolution fusion | flops 14504951808 | bytes 28311552 | tf_op jit(solution)/shard_map/ecd,efd->ecf/dot_general | solution.py:99
  249.9 84.0 %all-to-all-done.3 = bf16[8,384,768]{2,1,0:T(8,128)(2,1)} async-done(((bf16[8,384,768]{2,1,0:T(8,128)(2,1)}), bf16[8,384,768]{2,1,0:T(8,128)(2,1)}, u32[]{:S(2)}, u32[]{:S(2)}) %all-to-all-start.3) | async-done | bytes 4718624 | tf_op jit(solution)/shard_map/all_to_all | solution.py:134
  333.9 22.6 %fusion.18 = f32[3072,3072]{1,0:T(8,128)} fusion(bf16[3072,768]{1,0:T(8,128)(2,1)} %bitcast.17, bf16[1,768,3072]{2,1,0:T(8,128)(2,1)} %param.32), kind=kOutput, calls=%fused_computation.62 | convolution fusion | flops 14495514624 | bytes 47185920 | tf_op jit(solution)/shard_map/ecd,edf->ecf/dot_general | solution.py:89
  356.5 55.1 %fusion.7 = (bf16[3072,3072]{1,0:T(8,128)(2,1)}, bf16[3072,3072]{1,0:T(8,128)(2,1)}, f32[3072,3072]{1,0:T(8,128)}) fusion(bf16[3072,3072]{1,0:T(8,128)(2,1)} %convolution_convert_fusion, f32[3072,3072]{1,0:T(8,128)} %fusion.18, bf16[3072,768]{1,0:T(8,128)(2,1)} %bitcast.17, bf16[1,768,3072]{2,1,0:T(8,128)(2,1)} %param.31), kind=kOutput, calls=%fused_computation.17 | convolution fusion | flops 14627635200 | bytes 141557760 | tf_op jit(solution)/shard_map/ecd,edf->ecf/dot_general | solution.py:88
  411.6 21.2 %fusion.22 = f32[3072,768]{1,0:T(8,128)} fusion(bf16[3072,3072]{1,0:T(8,128)(2,1)} %get-tuple-element.16, bf16[1,768,3072]{2,1,0:T(8,128)(2,1)} %param.31), kind=kOutput, calls=%fused_computation.65 | convolution fusion | flops 14495514624 | bytes 33030144 | tf_op jit(solution)/shard_map/ecf,edf->ecd/dot_general | solution.py:105
  432.7 19.0 %fusion.33 = bf16[1,3072,768]{2,1,0:T(8,128)(2,1)S(1)} fusion(f32[3072,768]{1,0:T(8,128)} %fusion.22, bf16[3072,3072]{1,0:T(8,128)(2,1)} %get-tuple-element.15, bf16[1,768,3072]{2,1,0:T(8,128)(2,1)S(1)} %copy-done.51), kind=kOutput, calls=%fused_computation.75 | convolution fusion | flops 14500233216 | bytes 37748736 | tf_op jit(solution)/shard_map/ecf,edf->ecd/dot_general | solution.py:105
  451.8 67.0 %copy.190 = bf16[1,3072,768]{2,0,1:T(2,128)(2,1)} copy(bf16[1,3072,768]{2,1,0:T(8,128)(2,1)S(1)} %fusion.33) | data formatting | bytes 9437184 | tf_op jit(solution)/shard_map/convert_element_type | solution.py:105
  519.3 49.0 %reduce.5 = bf16[3072,768]{1,0:T(8,128)(2,1)} reduce(bf16[3072,1,768]{2,1,0:T(2,128)(2,1)} %bitcast.177, bf16[]{:T(256)} %broadcast.259), dimensions={1}, to_apply=%bitcast.172.reduce_sub_computation | reduce | bytes 9437186
  624.3 61.1 %all-to-all-done.4 = bf16[8,2,147456]{2,1,0:T(2,128)(2,1)} async-done(((bf16[8,2,147456]{2,1,0:T(2,128)(2,1)}), bf16[8,2,147456]{2,1,0:T(2,128)(2,1)}, u32[]{:S(2)}, u32[]{:S(2)}) %all-to-all-start.4) | async-done | bytes 4718624 | tf_op jit(solution)/shard_map/all_to_all | solution.py:139
  716.6 13.6 %gather_fusion = bf16[3072,768]{1,0:T(8,128)(2,1)} fusion(bf16[1025,768]{1,0:T(8,128)(2,1)S(1)} %concatenate.15, s32[3072]{0:T(1024)S(1)} %fusion.106), kind=kCustom, calls=%fused_computation.clone | custom fusion | bytes 9449472 | tf_op jit(solution)/shard_map/jit(_take)/gather | solution.py:75
  740.4 32.0 %fusion.11 = f32[1,3072,768]{2,1,0:T(8,128)} fusion(bf16[3072,768]{1,0:T(8,128)(2,1)} %bitcast.194, f32[3072,3072]{1,0:T(8,128)} %fusion.18, f32[3072,3072]{1,0:T(8,128)} %get-tuple-element.31), kind=kOutput, calls=%fused_computation.41 | convolution fusion | flops 14552137728 | bytes 89653248 | tf_op jit(solution)/shard_map/ecf,ecd->efd/dot_general | solution.py:98
  792.7 11.9 fusion.95
  808.8 11.3 fusion.98
  830.0 15.4 %all-to-all-done = bf16[8,384,768]{2,1,0:T(8,128)(2,1)} async-done(((bf16[8,384,768]{2,1,0:T(8,128)(2,1)}), bf16[8,384,768]{2,1,0:T(8,128)(2,1)}, u32[]{:S(2)}, u32[]{:S(2)}) %all-to-all-start) | async-done | bytes 4718624 | tf_op jit(solution)/shard_map/all_to_all | solution.py:126
  845.3 22.6 %fusion.26 = f32[3072,3072]{1,0:T(8,128)} fusion(bf16[3072,768]{1,0:T(8,128)(2,1)} %bitcast.3, bf16[1,768,3072]{2,1,0:T(8,128)(2,1)} %param.31), kind=kOutput, calls=%fused_computation.69 | convolution fusion | flops 14495514624 | bytes 47185920 | tf_op jit(solution)/shard_map/ecd,edf->ecf/dot_general | solution.py:88
  867.9 38.6 %fusion.28 = bf16[1,3072,768]{2,1,0:T(8,128)(2,1)} fusion(bf16[1,3072,768]{2,1,0:T(8,128)(2,1)} %param.33, f32[3072,3072]{1,0:T(8,128)} %fusion.26, bf16[3072,768]{1,0:T(8,128)(2,1)} %bitcast.3, bf16[1,768,3072]{2,1,0:T(8,128)(2,1)} %param.32), kind=kOutput, calls=%fused_computation.74 | convolution fusion | flops 29050011648 | bytes 56623104 | tf_op jit(solution)/shard_map/ecf,efd->ecd/dot_general | solution.py:94
  906.6 9.5 copy.191
  916.1 49.0 %reduce.6 = bf16[3072,768]{1,0:T(8,128)(2,1)} reduce(bf16[3072,1,768]{2,1,0:T(2,128)(2,1)} %bitcast.178, bf16[]{:T(256)} %broadcast.259), dimensions={1}, to_apply=%bitcast.173.reduce_sub_computation | reduce | bytes 9437186
  986.9 21.2 %convolution_bitcast_fusion = f32[1,768,3072]{2,1,0:T(8,128)} fusion(bf16[3072,768]{1,0:T(8,128)(2,1)} %bitcast.17, bf16[3072,3072]{1,0:T(8,128)(2,1)} %get-tuple-element.15), kind=kOutput, calls=%fused_computation.39 | convolution fusion | flops 14495514624 | bytes 33030144 | tf_op jit(solution)/shard_map/ecd,ecf->edf/dot_general | solution.py:104
  1008.1 21.5 %convolution_bitcast_fusion.1 = f32[1,768,3072]{2,1,0:T(8,128)} fusion(bf16[3072,768]{1,0:T(8,128)(2,1)} %bitcast.17, bf16[3072,3072]{1,0:T(8,128)(2,1)} %get-tuple-element.16), kind=kOutput, calls=%fused_computation.40 | convolution fusion | flops 14495514624 | bytes 33030144 | tf_op jit(solution)/shard_map/ecd,ecf->edf/dot_general | solution.py:103
  1037.2 230.3 %all-reduce.7.cloned.1.call-done = f32[4,768,768]{2,1,0:T(8,128)} async-done(((f32[4,768,768]{2,1,0:T(8,128)}), f32[4,768,768]{2,1,0:T(8,128)}) %all-reduce.7.cloned.1.call-update) | async-done | bytes 9437200 | tf_op jit(solution)/shard_map/psum | solution.py:143
  (210 shorter events, 277.4 us)
Async XLA Ops:
  7.2 64.3 %copy-start = (bf16[768,768]{1,0:T(8,128)(2,1)S(1)}, bf16[768,768]{1,0:T(8,128)(2,1)}, u32[]{:S(2)}) copy-start(bf16[768,768]{1,0:T(8,128)(2,1)} %param.28) | copy-start | bytes 3538948
  8.6 15.2 %copy-start.37 = (s32[1024,1]{0,1:T(1,128)}, s32[1024,1]{0,1:T(1,128)S(1)}, u32[]{:S(2)}) copy-start(s32[1024,1]{0,1:T(1,128)S(1)} %get-tuple-element.12) | copy-start | bytes 12292
  13.0 45.8 %copy-start.26 = (pred[256,256]{0,1:T(8,128)(4,1)}, pred[256,256]{0,1:T(8,128)(4,1)S(1)}, u32[]{:S(2)}) copy-start(pred[256,256]{0,1:T(8,128)(4,1)S(1)} %iota_compare_fusion) | copy-start | bytes 196612
  15.4 33.5 %copy-start.42 = (f32[1024]{0:T(1024)}, f32[1024]{0:T(1024)S(1)}, u32[]{:S(2)}) copy-start(f32[1024]{0:T(1024)S(1)} %fusion.114) | copy-start | bytes 12292
  28.1 8.5 copy-start.4
  28.1 8.5 copy-start.39
  89.6 16.2 %slice-start = ((bf16[3073]{0:T(1024)(128)(2,1)}), bf16[3072]{0:T(1024)(128)(2,1)S(1)}, s32[]{:S(2)}) async-start(bf16[3073]{0:T(1024)(128)(2,1)} %copy-done.34), calls=%async_computation.6 | async-start | bytes 12288 | tf_op jit(solution)/shard_map/slice | solution.py:66
  224.2 109.7 %all-to-all-start.3 = ((bf16[8,384,768]{2,1,0:T(8,128)(2,1)}), bf16[8,384,768]{2,1,0:T(8,128)(2,1)}, u32[]{:S(2)}, u32[]{:S(2)}) async-start(bf16[8,384,768]{2,1,0:T(8,128)(2,1)} %bitcast.184), calls=%async_computation.3 | async-start | bytes 9437184 | tf_op jit(solution)/shard_map/all_to_all | solution.py:134
  411.6 21.2 %copy-start.51 = (bf16[1,768,3072]{2,1,0:T(8,128)(2,1)S(1)}, bf16[1,768,3072]{2,1,0:T(8,128)(2,1)}, u32[]{:S(2)}) copy-start(bf16[1,768,3072]{2,1,0:T(8,128)(2,1)} %param.32) | copy-start | bytes 14155780
  575.5 109.9 %all-to-all-start.4 = ((bf16[8,2,147456]{2,1,0:T(2,128)(2,1)}), bf16[8,2,147456]{2,1,0:T(2,128)(2,1)}, u32[]{:S(2)}, u32[]{:S(2)}) async-start(bf16[8,2,147456]{2,1,0:T(2,128)(2,1)} %reshape.423), calls=%async_computation.4 | async-start | bytes 9437184 | tf_op jit(solution)/shard_map/all_to_all | solution.py:139
  611.4 8.7 copy-start.38
  611.4 8.8 copy-start.19
  701.6 8.7 copy-start.2
  701.6 8.7 copy-start.29
  701.6 8.7 copy-start.46
  735.8 109.5 %all-to-all-start = ((bf16[8,384,768]{2,1,0:T(8,128)(2,1)}), bf16[8,384,768]{2,1,0:T(8,128)(2,1)}, u32[]{:S(2)}, u32[]{:S(2)}) async-start(bf16[8,384,768]{2,1,0:T(8,128)(2,1)} %bitcast.183), calls=%async_computation | async-start | bytes 9437184 | tf_op jit(solution)/shard_map/all_to_all | solution.py:126
  740.4 32.0 %copy-start.10 = (bf16[1024,768]{1,0:T(8,128)(2,1)S(1)}, bf16[1024,768]{1,0:T(8,128)(2,1)}, u32[]{:S(2)}) copy-start(bf16[1024,768]{1,0:T(8,128)(2,1)} %get-tuple-element.21) | copy-start | bytes 4718596
  972.3 302.7 %all-to-all-start.1 = ((bf16[8,2,147456]{2,1,0:T(2,128)(2,1)}), bf16[8,2,147456]{2,1,0:T(2,128)(2,1)}, u32[]{:S(2)}, u32[]{:S(2)}) async-start(bf16[8,2,147456]{2,1,0:T(2,128)(2,1)} %reshape.421), calls=%async_computation.1 | async-start | bytes 9437184 | tf_op jit(solution)/shard_map/all_to_all | solution.py:128
  976.9 290.6 %all-reduce.7.cloned.1.call-start = ((), (), s32[]{:S(2)}) async-start(), calls=%async_computation.5 | async-start | bytes 18874368 | tf_op jit(solution)/shard_map/psum | solution.py:143
  1008.1 21.5 %copy-start.24 = (bf16[96,8,4,256]{3,1,2,0:T(8,128)(2,1)S(1)}, bf16[96,8,4,256]{3,1,2,0:T(8,128)(2,1)}, u32[]{:S(2)}) copy-start(bf16[96,8,4,256]{3,1,2,0:T(8,128)(2,1)} %copy-done.23) | copy-start | bytes 4718596
  1008.1 21.5 %copy-start.52 = (bf16[768,768]{1,0:T(8,128)(2,1)S(1)}, bf16[768,768]{1,0:T(8,128)(2,1)}, u32[]{:S(2)}) copy-start(bf16[768,768]{1,0:T(8,128)(2,1)} %param.25) | copy-start | bytes 3538948
  1291.4 8.7 copy-start.9
  1291.4 8.7 copy-start.44
  1291.4 8.7 copy-start.47
  (38 other events, 105.3 us)
Sparse Core Ops, SparseCore 0:
  987.0 280.4 all-reduce.6
where the time goes:
time: 1320 us; the launch traced here: 1310 us
  waiting for transfers between devices  391 us (30%)
  matrix products  369 us (28%)
  local copies, waits for them, and re-layouts  270 us (20%)
  other arithmetic  134 us (10%)
  blocking collectives  111 us (8%)
  starting transfers between devices  19.2 us (1%)
  between operations  15.1 us (1%)
    psum x1, waiting for transfers between devices, device_program(): attn_grads = lax.psum(attn_grads, 'ep')  230 us
    all_to_all x1, blocking collectives, device_program(): d_out_b = lax.all_to_all(d_send, 'ep', 0, 1, tiled=True)  111 us
    unnamed x3, other arithmetic  98.7 us
    all_to_all x1, waiting for transfers between devices, device_program(): lax.all_to_all(dispatch(u_b, inv_tok_b, num_experts, slot_count), 'ep', 0...  84 us
    dot_general x2, matrix products, expert_hidden(): jnp.einsum('ecd,edf->ecf', expert_in, w_gate, preferred_element_type=jnp....  77.7 us
    convert_element_type x1, local copies, waits for them, and re-layouts, expert_backward(): (jnp.einsum('ecf,edf->ecd', d_zgate, w_gate, preferred_element_type=jnp.f...  67 us
    all_to_all x1, waiting for transfers between devices, device_program(): d_back = lax.all_to_all(d_in_b, 'ep', 1, 0, tiled=True)  61.1 us
    unnamed x124, local copies, waits for them, and re-layouts  50.8 us
  transfers between devices with their start and end apart: 5, of which 4 were waited for; matrix products, arithmetic and copies ran while one was open for 17% of the time, Pallas kernels for 0%

commit v1 on v0

v1 whole, which is shorter than its diff:
```python
import functools

import jax
import jax.numpy as jnp
from jax import lax
from jax.experimental import pallas as pl
from jax.experimental.pallas import tpu as pltpu
from jax.sharding import PartitionSpec as P

RMS_EPS = 1e-6
HEAD_DIM = 128
SEQ_MAX = 256
FAR = 1 << 20
BF = jnp.bfloat16
F32 = jnp.float32
VMEM_LIMIT = 60 * 1024 * 1024


def capacity_of(tokens, choices, num_experts):
    return ((3 * tokens * choices // num_experts + 7) // 8) * 8


def mm(lhs, rhs):
    return jnp.dot(lhs, rhs, preferred_element_type=F32)


def mm_nt(lhs, rhs):
    return lax.dot_general(lhs, rhs, (((1,), (1,)), ((), ())), preferred_element_type=F32)


def mm_tn(lhs, rhs):
    return lax.dot_general(lhs, rhs, (((0,), (0,)), ((), ())), preferred_element_type=F32)


def inv_rms_of(rows_f):
    return lax.rsqrt(jnp.mean(rows_f * rows_f, axis=-1, keepdims=True) + RMS_EPS)


def norm_rows(rows_f, gain_row):
    return (rows_f * inv_rms_of(rows_f) * gain_row).astype(BF)


def norm_back(rows_f, gain_row, d_normed):
    inv = inv_rms_of(rows_f)
    scaled = d_normed.astype(F32) * gain_row
    dot_mean = jnp.mean(scaled * rows_f, axis=-1, keepdims=True)
    return (scaled * inv - rows_f * (inv * inv * inv * dot_mean)).astype(BF)


def pack_rows(pos_row, src_ref, dst_ref, chunk):
    tokens = pos_row.shape[1]

    def body(c, carry):
        base = pl.multiple_of(c * chunk, chunk)
        want = base + lax.broadcasted_iota(jnp.int32, (chunk, tokens), 0)
        onehot = jnp.where(want == pos_row, 1.0, 0.0).astype(BF)
        dst_ref[pl.ds(base, chunk), :] = mm(onehot, src_ref[...]).astype(BF)
        return carry

    lax.fori_loop(0, dst_ref.shape[0] // chunk, body, 0)


def unpack_rows(pos_col, num_experts, back_ref):
    seg = back_ref.shape[0] // num_experts
    total = jnp.zeros((pos_col.shape[0], back_ref.shape[1]), F32)
    for e in range(num_experts):
        want = e * seg + lax.broadcasted_iota(jnp.int32, (pos_col.shape[0], seg), 1)
        total += mm(jnp.where(want == pos_col, 1.0, 0.0).astype(BF), back_ref[pl.ds(e * seg, seg), :])
    return total


def route_one(e_ref, s_ref, pos_ref, num_experts, seg):
    tokens = e_ref.shape[1]
    expert = e_ref[...]
    kept = s_ref[...] >= 0
    lane_expert = lax.broadcasted_iota(jnp.int32, (num_experts, tokens), 0)
    onehot_f = jnp.where((lane_expert == expert) & kept, 1.0, 0.0)
    onehot = onehot_f.astype(BF)
    before = lax.broadcasted_iota(jnp.int32, (tokens, tokens), 0) < lax.broadcasted_iota(jnp.int32, (tokens, tokens), 1)
    rank = mm(onehot, jnp.where(before, 1.0, 0.0).astype(BF))
    pos = expert * seg + jnp.sum(onehot_f * rank, axis=0, keepdims=True).astype(jnp.int32)
    pos = jnp.where(kept, pos, FAR)
    pos_ref[...] = pos
    return pos


def route_kernel(num_experts, ea_ref, sa_ref, eb_ref, sb_ref, gate_ref, dy_ref, pos_a_ref, pos_b_ref, d_pack_ref, scaled):
    seg = d_pack_ref.shape[0] // num_experts
    route_one(ea_ref, sa_ref, pos_a_ref, num_experts, seg)
    pos_b = route_one(eb_ref, sb_ref, pos_b_ref, num_experts, seg)
    scaled[...] = (dy_ref[...].astype(F32) * gate_ref[...].astype(F32)).astype(BF)
    pack_rows(pos_b, scaled, d_pack_ref, seg)


def route(expert_a, slot_a, expert_b, slot_b, gate_b, dy_b, num_experts, seg):
    tokens, hidden = dy_b.shape
    row = jax.ShapeDtypeStruct((1, tokens), jnp.int32)
    return pl.pallas_call(
        functools.partial(route_kernel, num_experts),
        out_shape=(row, row, jax.ShapeDtypeStruct((num_experts * seg, hidden), BF)),
        scratch_shapes=[pltpu.VMEM((tokens, hidden), BF)],
        compiler_params=pltpu.CompilerParams(vmem_limit_bytes=VMEM_LIMIT),
        cost_estimate=pl.CostEstimate(flops=4 * tokens * tokens * hidden, bytes_accessed=2 * 2 * tokens * hidden, transcendentals=0),
        name='route',
    )(expert_a.reshape(1, tokens), slot_a.reshape(1, tokens), expert_b.reshape(1, tokens), slot_b.reshape(1, tokens), gate_b, dy_b)


def softmax_head(q_head, k_head, causal):
    scores = jnp.where(causal, mm_nt(q_head, k_head) * HEAD_DIM ** -0.5, -1e30)
    expd = jnp.exp(scores - jnp.max(scores, axis=-1, keepdims=True))
    return expd * (1.0 / jnp.sum(expd, axis=-1, keepdims=True))


def causal_mask(seq_len):
    return lax.broadcasted_iota(jnp.int32, (seq_len, seq_len), 0) >= lax.broadcasted_iota(jnp.int32, (seq_len, seq_len), 1)


def attn_kernel(chunk, x_ref, wq_ref, wk_ref, wv_ref, wo_ref, ga_ref, gm_ref, pos_ref, h_ref, pack_ref, *rest):
    q_ref, k_ref, v_ref, mixed_ref, u_all = rest
    seq_len, hidden = x_ref.shape
    x_f = x_ref[...].astype(F32)
    normed = norm_rows(x_f, ga_ref[...])
    q_ref[...] = mm(normed, wq_ref[...]).astype(BF)
    k_ref[...] = mm(normed, wk_ref[...]).astype(BF)
    v_ref[...] = mm(normed, wv_ref[...]).astype(BF)
    causal = causal_mask(seq_len)
    for head in range(hidden // HEAD_DIM):
        cols = pl.ds(head * HEAD_DIM, HEAD_DIM)
        probs = softmax_head(q_ref[:, cols], k_ref[:, cols], causal).astype(BF)
        mixed_ref[:, cols] = mm(probs, v_ref[:, cols]).astype(BF)
    h_rows = (x_f + mm(mixed_ref[...], wo_ref[...])).astype(BF)
    h_ref[...] = h_rows
    step = pl.program_id(0)
    u_all[pl.ds(pl.multiple_of(step * seq_len, seq_len), seq_len), :] = norm_rows(h_rows.astype(F32), gm_ref[...])

    @pl.when(step == pl.num_programs(0) - 1)
    def _():
        pack_rows(pos_ref[...], u_all, pack_ref, chunk)


def attn_forward(x_rows, w_q, w_k, w_v, w_o, gain_attn, gain_moe, pos_row, keep, num_experts, seg):
    tokens, hidden = x_rows.shape
    seq_len = min(tokens, SEQ_MAX)
    seqs = tokens // seq_len
    rows = pl.BlockSpec((seq_len, hidden), lambda i: (i, 0))
    whole = pl.BlockSpec((hidden, hidden), lambda i: (0, 0))
    gain = pl.BlockSpec((1, hidden), lambda i: (0, 0))
    full = jax.ShapeDtypeStruct((tokens, hidden), BF)
    out_shape = [full, jax.ShapeDtypeStruct((num_experts * seg, hidden), BF)]
    out_specs = [rows, pl.BlockSpec((num_experts * seg, hidden), lambda i: (0, 0))]
    scratch = [pltpu.VMEM((tokens, hidden), BF)]
    if keep:
        out_shape += [full] * 4
        out_specs += [rows] * 4
    else:
        scratch = [pltpu.VMEM((seq_len, hidden), BF)] * 4 + scratch
    return pl.pallas_call(
        functools.partial(attn_kernel, seg),
        grid=(seqs,),
        in_specs=[rows, whole, whole, whole, whole, gain, gain, pl.BlockSpec((1, tokens), lambda i: (0, 0))],
        out_specs=out_specs,
        out_shape=out_shape,
        scratch_shapes=scratch,
        compiler_params=pltpu.CompilerParams(vmem_limit_bytes=VMEM_LIMIT, dimension_semantics=('arbitrary',)),
        cost_estimate=pl.CostEstimate(flops=14 * tokens * hidden * hidden, bytes_accessed=20 * tokens * hidden, transcendentals=tokens * seq_len * 6),
        name='attn_fwd_keep' if keep else 'attn_fwd',
    )(x_rows, w_q, w_k, w_v, w_o, gain_attn[None, :], gain_moe[None, :], pos_row)


def weight_specs(hidden, ff):
    up = pl.BlockSpec((hidden, ff), lambda i, n, ids: (0, 0), pipeline_mode=pl.Buffered(1))
    down = pl.BlockSpec((ff, hidden), lambda i, n, ids: (0, 0), pipeline_mode=pl.Buffered(1))
    return [up, up, down]


def pick_specs(half, hidden):
    def picked(part):
        return pl.BlockSpec((half, hidden), lambda i, n, ids: (ids[jnp.minimum(2 * i + part, jnp.maximum(n[0] - 1, 0))], 0))

    return [picked(0), picked(1)]


def join_pair(first_ref, second_ref, both):
    second = second_ref[...]
    return jnp.concatenate([first_ref[...], jnp.where(both, second, jnp.zeros_like(second))], axis=0)


def pair_loop(n_ref, ids_ref, buf, out_ref, sem, half, compute):
    step = pl.program_id(0)
    steps = pl.num_programs(0)

    def copies(at):
        slot = lax.rem(at, 2)
        return [
            pltpu.make_async_copy(
                buf.at[slot, pl.ds(part * half, half), :],
                out_ref.at[pl.ds(pl.multiple_of(ids_ref[2 * at + part] * half, half), half), :],
                sem.at[slot, part],
            )
            for part in range(2)
        ]

    def drain(at):
        for copy in copies(at):
            copy.wait()

    @pl.when(step >= 2)
    def _():
        drain(step - 2)

    dst = buf.at[lax.rem(step, 2)]

    @pl.when(2 * step < n_ref[0])
    def _():
        compute(2 * step + 1 < n_ref[0], dst)

    @pl.when(2 * step >= n_ref[0])
    def _():
        dst[...] = jnp.zeros_like(dst)

    for copy in copies(step):
        copy.start()

    @pl.when(step == steps - 1)
    def _():
        drain(step - 1)
        drain(step)


def ffn_fwd_kernel(half, chunk, n_ref, ids_ref, u0_ref, u1_ref, wg_ref, wu_ref, wd_ref, o_ref, acc, buf, sem):
    def compute(both, dst):
        u_rows = join_pair(u0_ref, u1_ref, both)
        acc[...] = jnp.zeros_like(acc)

        def body(c, carry):
            cols = pl.ds(pl.multiple_of(c * chunk, chunk), chunk)
            z_gate = mm(u_rows, wg_ref[:, cols])
            z_up = mm(u_rows, wu_ref[:, cols])
            act = (z_gate * jax.nn.sigmoid(z_gate) * z_up).astype(BF)
            acc[...] += mm(act, wd_ref[cols, :])
            return carry

        lax.fori_loop(0, wg_ref.shape[1] // chunk, body, 0)
        dst[...] = acc[...].astype(BF)

    pair_loop(n_ref, ids_ref, buf, o_ref, sem, half, compute)


def pair_scratch(half, hidden):
    return [pltpu.VMEM((2 * half, hidden), F32), pltpu.VMEM((2, 2 * half, hidden), BF), pltpu.SemaphoreType.DMA((2, 2))]


def ffn_forward(n_blocks, ids, u_rows, w_gate, w_up, w_down, half=128, chunk=512):
    rows, hidden = u_rows.shape
    ff = w_gate.shape[1]
    return pl.pallas_call(
        functools.partial(ffn_fwd_kernel, half, chunk),
        grid_spec=pltpu.PrefetchScalarGridSpec(
            num_scalar_prefetch=2,
            grid=(rows // (2 * half),),
            in_specs=pick_specs(half, hidden) + weight_specs(hidden, ff),
            out_specs=pl.BlockSpec(memory_space=pl.ANY),
            scratch_shapes=pair_scratch(half, hidden),
        ),
        out_shape=jax.ShapeDtypeStruct((rows, hidden), BF),
        compiler_params=pltpu.CompilerParams(vmem_limit_bytes=VMEM_LIMIT, dimension_semantics=('arbitrary',)),
        cost_estimate=pl.CostEstimate(flops=3 * rows * hidden * ff, bytes_accessed=6 * hidden * ff, transcendentals=0),
        name='ffn_fwd',
    )(n_blocks, ids, u_rows, u_rows, w_gate, w_up, w_down)


def ffn_bwd_kernel(half, chunk, n_ref, ids_ref, u0_ref, u1_ref, d0_ref, d1_ref, wg_ref, wu_ref, wd_ref, din_ref, uc_ref, dc_ref, act_ref, dzg_ref, dzu_ref, acc, buf, sem):
    def compute(both, dst):
        u_rows = join_pair(u0_ref, u1_ref, both)
        d_out = join_pair(d0_ref, d1_ref, both)
        uc_ref[...] = u_rows
        dc_ref[...] = d_out
        acc[...] = jnp.zeros_like(acc)

        def body(c, carry):
            cols = pl.ds(pl.multiple_of(c * chunk, chunk), chunk)
            z_gate = mm(u_rows, wg_ref[:, cols])
            z_up = mm(u_rows, wu_ref[:, cols])
            d_act = mm_nt(d_out, wd_ref[cols, :]).astype(BF).astype(F32)
            sig = jax.nn.sigmoid(z_gate)
            silu = z_gate * sig
            act_ref[:, cols] = (silu * z_up).astype(BF)
            d_zg = (d_act * z_up * sig * (1.0 + z_gate * (1.0 - sig))).astype(BF)
            d_zu = (d_act * silu).astype(BF)
            dzg_ref[:, cols] = d_zg
            dzu_ref[:, cols] = d_zu
            acc[...] += mm_nt(d_zg, wg_ref[:, cols]) + mm_nt(d_zu, wu_ref[:, cols])
            return carry

        lax.fori_loop(0, wg_ref.shape[1] // chunk, body, 0)
        dst[...] = acc[...].astype(BF)

    pair_loop(n_ref, ids_ref, buf, din_ref, sem, half, compute)


def step_index(n_ref, i):
    return jnp.minimum(i, jnp.maximum((n_ref[0] + 1) // 2 - 1, 0))


def ffn_backward(n_blocks, ids, u_rows, d_out, w_gate, w_up, w_down, half=128, chunk=512):
    rows, hidden = u_rows.shape
    ff = w_gate.shape[1]
    row_spec = pl.BlockSpec((2 * half, hidden), lambda i, n, ids: (step_index(n, i), 0))
    wide_spec = pl.BlockSpec((2 * half, ff), lambda i, n, ids: (step_index(n, i), 0))
    thin, wide = jax.ShapeDtypeStruct((rows, hidden), BF), jax.ShapeDtypeStruct((rows, ff), BF)
    return pl.pallas_call(
        functools.partial(ffn_bwd_kernel, half, chunk),
        grid_spec=pltpu.PrefetchScalarGridSpec(
            num_scalar_prefetch=2,
            grid=(rows // (2 * half),),
            in_specs=pick_specs(half, hidden) + pick_specs(half, hidden) + weight_specs(hidden, ff),
            out_specs=[pl.BlockSpec(memory_space=pl.ANY), row_spec, row_spec, wide_spec, wide_spec, wide_spec],
            scratch_shapes=pair_scratch(half, hidden),
        ),
        out_shape=(thin, thin, thin, wide, wide, wide),
        compiler_params=pltpu.CompilerParams(vmem_limit_bytes=VMEM_LIMIT, dimension_semantics=('arbitrary',)),
        cost_estimate=pl.CostEstimate(flops=6 * rows * hidden * ff, bytes_accessed=6 * hidden * ff + 3 * rows * ff, transcendentals=0),
        name='ffn_bwd',
    )(n_blocks, ids, u_rows, u_rows, d_out, d_out, w_gate, w_up, w_down)


def ffn_grad_kernel(n_ref, u_ref, d_ref, act_ref, dzg_ref, dzu_ref, dwg_ref, dwu_ref, dwd_ref):
    step = pl.program_id(1)

    @pl.when(step == 0)
    def _():
        dwg_ref[...] = jnp.zeros_like(dwg_ref)
        dwu_ref[...] = jnp.zeros_like(dwu_ref)
        dwd_ref[...] = jnp.zeros_like(dwd_ref)

    @pl.when(2 * step < n_ref[0])
    def _():
        dwg_ref[...] += mm_tn(u_ref[...], dzg_ref[...])
        dwu_ref[...] += mm_tn(u_ref[...], dzu_ref[...])
        dwd_ref[...] += mm_tn(act_ref[...], d_ref[...])


def ffn_grads(n_blocks, u_rows, d_out, act, d_zg, d_zu, block=256, chunk=1024):
    rows, hidden = u_rows.shape
    ff = act.shape[1]
    row_spec = pl.BlockSpec((block, hidden), lambda j, i, n: (step_index(n, i), 0))
    wide_spec = pl.BlockSpec((block, chunk), lambda j, i, n: (step_index(n, i), j))
    up_spec = pl.BlockSpec((hidden, chunk), lambda j, i, n: (0, j))
    down_spec = pl.BlockSpec((chunk, hidden), lambda j, i, n: (j, 0))
    return pl.pallas_call(
        ffn_grad_kernel,
        grid_spec=pltpu.PrefetchScalarGridSpec(
            num_scalar_prefetch=1,
            grid=(ff // chunk, rows // block),
            in_specs=[row_spec, row_spec, wide_spec, wide_spec, wide_spec],
            out_specs=[up_spec, up_spec, down_spec],
        ),
        out_shape=(jax.ShapeDtypeStruct((hidden, ff), F32), jax.ShapeDtypeStruct((hidden, ff), F32), jax.ShapeDtypeStruct((ff, hidden), F32)),
        compiler_params=pltpu.CompilerParams(vmem_limit_bytes=VMEM_LIMIT, dimension_semantics=('arbitrary', 'arbitrary')),
        cost_estimate=pl.CostEstimate(flops=3 * rows * hidden * ff, bytes_accessed=12 * hidden * ff + 3 * rows * ff, transcendentals=0),
        name='ffn_grads',
    )(n_blocks, u_rows, d_out, act, d_zg, d_zu)


def attn_bwd_kernel(num_experts, x_ref, h_ref, dy_ref, q_ref, k_ref, v_ref, mixed_ref, back_ref, pos_ref, wq_ref, wk_ref, wv_ref, wo_ref, ga_ref, gm_ref, dx_ref, dw_ref, dq, dk, dv, dmix):
    seq_len, hidden = x_ref.shape
    d_u = unpack_rows(pos_ref[...], num_experts, back_ref).astype(BF)
    d_h = (dy_ref[...].astype(F32) + norm_back(h_ref[...].astype(F32), gm_ref[...], d_u).astype(F32)).astype(BF)
    dmix[...] = mm_nt(d_h, wo_ref[...]).astype(BF)
    causal = causal_mask(seq_len)
    for head in range(hidden // HEAD_DIM):
        cols = pl.ds(head * HEAD_DIM, HEAD_DIM)
        q_head, k_head, v_head, d_mixed = q_ref[:, cols], k_ref[:, cols], v_ref[:, cols], dmix[:, cols]
        probs = softmax_head(q_head, k_head, causal)
        d_probs = mm_nt(d_mixed, v_head)
        dv[:, cols] = mm_tn(probs.astype(BF), d_mixed).astype(BF)
        d_scores = (probs * (d_probs - jnp.sum(d_probs * probs, axis=-1, keepdims=True)) * HEAD_DIM ** -0.5).astype(BF)
        dq[:, cols] = mm(d_scores, k_head).astype(BF)
        dk[:, cols] = mm_tn(d_scores, q_head).astype(BF)
    x_f = x_ref[...].astype(F32)
    normed = norm_rows(x_f, ga_ref[...])

    @pl.when(pl.program_id(0) == 0)
    def _():
        dw_ref[...] = jnp.zeros_like(dw_ref)

    normed_t = normed.T
    dw_ref[0] += mm(normed_t, dq[...])
    dw_ref[1] += mm(normed_t, dk[...])
    dw_ref[2] += mm(normed_t, dv[...])
    dw_ref[3] += mm_tn(mixed_ref[...], d_h)
    d_normed = (mm_nt(dq[...], wq_ref[...]) + mm_nt(dk[...], wk_ref[...]) + mm_nt(dv[...], wv_ref[...])).astype(BF)
    dx_ref[...] = (d_h.astype(F32) + norm_back(x_f, ga_ref[...], d_normed).astype(F32)).astype(BF)


def attn_backward(num_experts, x_rows, h_rows, dy_rows, saved, back, pos_col, w_q, w_k, w_v, w_o, gain_attn, gain_moe):
    tokens, hidden = x_rows.shape
    seq_len = min(tokens, SEQ_MAX)
    rows = pl.BlockSpec((seq_len, hidden), lambda i: (i, 0))
    whole = pl.BlockSpec((hidden, hidden), lambda i: (0, 0))
    gain = pl.BlockSpec((1, hidden), lambda i: (0, 0))
    return pl.pallas_call(
        functools.partial(attn_bwd_kernel, num_experts),
        grid=(tokens // seq_len,),
        in_specs=[rows] * 7 + [pl.BlockSpec(back.shape, lambda i: (0, 0)), pl.BlockSpec((seq_len, 1), lambda i: (i, 0))] + [whole] * 4 + [gain] * 2,
        out_specs=[rows, pl.BlockSpec((4, hidden, hidden), lambda i: (0, 0, 0))],
        out_shape=(jax.ShapeDtypeStruct((tokens, hidden), BF), jax.ShapeDtypeStruct((4, hidden, hidden), F32)),
        scratch_shapes=[pltpu.VMEM((seq_len, hidden), BF)] * 4,
        compiler_params=pltpu.CompilerParams(vmem_limit_bytes=VMEM_LIMIT, dimension_semantics=('arbitrary',)),
        cost_estimate=pl.CostEstimate(flops=26 * tokens * hidden * hidden, bytes_accessed=40 * tokens * hidden, transcendentals=tokens * seq_len * 6),
        name='attn_bwd',
    )(x_rows, h_rows, dy_rows, *saved, back, pos_col, w_q, w_k, w_v, w_o, gain_attn[None, :], gain_moe[None, :])


def combine_kernel(num_experts, h_ref, back_ref, pos_ref, gate_ref, y_ref):
    picked = unpack_rows(pos_ref[...], num_experts, back_ref)
    y_ref[...] = (h_ref[...].astype(F32) + gate_ref[...].astype(F32) * picked).astype(BF)


def combine(num_experts, h_rows, back, pos_col, gate_col):
    tokens, hidden = h_rows.shape
    block = min(tokens, 256)
    rows = pl.BlockSpec((block, hidden), lambda i: (i, 0))
    one = pl.BlockSpec((block, 1), lambda i: (i, 0))
    return pl.pallas_call(
        functools.partial(combine_kernel, num_experts),
        grid=(tokens // block,),
        in_specs=[rows, pl.BlockSpec(back.shape, lambda i: (0, 0)), one, one],
        out_specs=rows,
        out_shape=jax.ShapeDtypeStruct((tokens, hidden), BF),
        compiler_params=pltpu.CompilerParams(vmem_limit_bytes=VMEM_LIMIT, dimension_semantics=('arbitrary',)),
        cost_estimate=pl.CostEstimate(flops=2 * tokens * tokens * hidden, bytes_accessed=6 * tokens * hidden, transcendentals=0),
        name='combine',
    )(h_rows, back, pos_col, gate_col)


def active_blocks(rows, half):
    blocks = rows.shape[0] // half
    flags = jnp.any(rows.reshape(blocks, half, rows.shape[1]) != 0, axis=(1, 2)).astype(jnp.int32)
    earlier = jnp.arange(blocks)[:, None] < jnp.arange(blocks)[None, :]
    total = jnp.sum(flags)
    rank_on = jnp.sum(jnp.where(earlier, flags[:, None], 0), axis=0)
    rank_off = total + jnp.sum(jnp.where(earlier, 1 - flags[:, None], 0), axis=0)
    rank = jnp.where(flags > 0, rank_on, rank_off)
    ids = jnp.sum(jnp.where(rank[None, :] == jnp.arange(blocks)[:, None], jnp.arange(blocks)[None, :], 0), axis=1)
    return total.astype(jnp.int32).reshape(1), ids.astype(jnp.int32)


CHUNK = 64
LAG_TOTAL = 3
LAG_FORWARD = 6


def reduce_kernel(x_ref, *rest):
    outs, (prt, acc, from_end, from_mid, tot, s_prt, r_prt, s_up, r_up, s_mid, r_mid, s_end, s_fwd, s_share, r_tot, r_share, s_out) = rest[:4], rest[4:]
    me = lax.axis_index('ep')
    core, z = lax.rem(me, 2), me // 2
    is_mid = (z == 1) | (z == 2)
    is_end = jnp.logical_not(is_mid)
    side = z // 2
    half = acc.shape[0]
    steps = half // CHUNK
    partner = 2 * z + 1 - core
    mate = 2 * (2 * side + 1 - lax.rem(z, 2)) + core
    across = 2 * (3 - z) + core

    def send(src, dst, send_sem, recv_sem, to):
        return pltpu.make_async_remote_copy(src_ref=src, dst_ref=dst, send_sem=send_sem, recv_sem=recv_sem, device_id={'ep': to}, device_id_type=pl.DeviceIdType.MESH)

    def rows(k):
        return pl.ds(pl.multiple_of(k * CHUNK, CHUNK), CHUNK)

    def mine(k):
        return pl.ds(pl.multiple_of(core * half + k * CHUNK, CHUNK), CHUNK)

    def theirs(k):
        return pl.ds(pl.multiple_of((1 - core) * half + k * CHUNK, CHUNK), CHUNK)

    def c_prt(k):
        return send(x_ref.at[theirs(k), :], prt.at[rows(k), :], s_prt.at[k], r_prt.at[k], partner)

    def c_up(k):
        return send(acc.at[rows(k), :], from_end.at[rows(k), :], s_up.at[k], r_up.at[k], mate)

    def c_mid(k):
        return send(acc.at[rows(k), :], from_mid.at[rows(k), :], s_mid.at[k], r_mid.at[k], across)

    def c_end(k):
        return send(tot.at[mine(k), :], tot.at[mine(k), :], s_end.at[k], r_tot.at[k], mate)

    def c_fwd(k):
        return send(tot.at[mine(k), :], tot.at[mine(k), :], s_fwd.at[k], r_tot.at[k], across)

    def c_share(k):
        return send(tot.at[mine(k), :], tot.at[mine(k), :], s_share.at[k], r_share.at[k], partner)

    barrier = pltpu.get_barrier_semaphore()
    for peer in (partner, mate):
        pl.semaphore_signal(barrier, inc=1, device_id={'ep': peer}, device_id_type=pl.DeviceIdType.MESH)

    @pl.when(is_mid)
    def _():
        pl.semaphore_signal(barrier, inc=1, device_id={'ep': across}, device_id_type=pl.DeviceIdType.MESH)
        pl.semaphore_wait(barrier, 3)

    @pl.when(is_end)
    def _():
        pl.semaphore_wait(barrier, 2)

    def begin(k, carry):
        c_prt(k).start()
        return carry

    lax.fori_loop(0, steps, begin, 0)

    def chip_sum(k):
        c_prt(k).wait_recv()
        acc[rows(k), :] = x_ref[mine(k), :] + prt[rows(k), :]

    @pl.when(is_end)
    def _():
        def up(k, carry):
            chip_sum(k)
            c_up(k).start()
            return carry

        lax.fori_loop(0, steps, up, 0)

        def take(k, carry):
            c_end(k).wait_recv()
            c_share(k).start()
            return carry

        lax.fori_loop(0, steps, take, 0)

    @pl.when(is_mid)
    def _():
        def run(t, carry):
            @pl.when(t < steps)
            def _():
                chip_sum(t)
                c_up(t).wait_recv()
                acc[rows(t), :] += from_end[rows(t), :]

                @pl.when(lax.rem(t, 2) != side)
                def _():
                    c_mid(t).start()

            j = t - LAG_TOTAL

            @pl.when((j >= 0) & (j < steps) & (lax.rem(j + 2, 2) == side))
            def _():
                c_mid(j).wait_recv()
                tot[mine(j), :] = acc[rows(j), :] + from_mid[rows(j), :]
                c_fwd(j).start()
                c_end(j).start()
                c_share(j).start()

            f = t - LAG_FORWARD

            @pl.when((f >= 0) & (lax.rem(f + 6, 2) != side))
            def _():
                c_fwd(f).wait_recv()
                c_end(f).start()
                c_share(f).start()

            return carry

        lax.fori_loop(0, steps + LAG_FORWARD, run, 0)

    def finish(k, carry):
        c_share(k).wait_recv()
        c_prt(k).wait_send()
        c_share(k).wait_send()

        @pl.when(is_end)
        def _():
            c_up(k).wait_send()

        @pl.when(is_mid)
        def _():
            c_end(k).wait_send()

            @pl.when(lax.rem(k, 2) != side)
            def _():
                c_mid(k).wait_send()

            @pl.when(lax.rem(k, 2) == side)
            def _():
                c_fwd(k).wait_send()

        return carry

    lax.fori_loop(0, steps, finish, 0)
    size = outs[0].shape[0]
    flushes = [pltpu.make_async_copy(tot.at[pl.ds(i * size, size), :], out, s_out.at[i]) for i, out in enumerate(outs)]
    for flush in flushes:
        flush.start()
    for flush in flushes:
        flush.wait()


def group_sum(stacked):
    count, size, hidden = stacked.shape
    total = count * size
    half = total // 2
    steps = half // CHUNK
    dma = pltpu.SemaphoreType.DMA((steps,))
    return pl.pallas_call(
        reduce_kernel,
        in_specs=[pl.BlockSpec(memory_space=pltpu.VMEM)],
        out_specs=[pl.BlockSpec(memory_space=pl.ANY)] * count,
        out_shape=[jax.ShapeDtypeStruct((size, hidden), F32)] * count,
        scratch_shapes=[pltpu.VMEM((half, hidden), F32)] * 4 + [pltpu.VMEM((total, hidden), F32)] + [dma] * 11 + [pltpu.SemaphoreType.DMA((count,))],
        compiler_params=pltpu.CompilerParams(vmem_limit_bytes=VMEM_LIMIT, collective_id=0, has_side_effects=True),
        cost_estimate=pl.CostEstimate(flops=10 ** 11, bytes_accessed=8 * total * hidden, transcendentals=0),
        name='group_sum',
    )(stacked.reshape(total, hidden))


def solution(mesh):
    group_size = mesh.shape['ep']
    row_spec = P(('dp', 'ep'), None)
    rep_two = P(None, None)
    rep_one = P(None)
    expert_spec = P('ep', None, None)
    grad_spec = P('dp', None)
    expert_grad_spec = P(('dp', 'ep'), None, None)

    def device_program(x_a, x_b, dy_b, w_q, w_k, w_v, w_o, gain_attn, gain_moe, w_gate, w_up, w_down, expert_a, slot_a, gate_a, expert_b, slot_b, gate_b):
        tokens, hidden = x_a.shape
        num_experts = group_size
        seg = capacity_of(tokens, 1, num_experts)
        half = seg // 3
        w_gate, w_up, w_down = w_gate[0], w_up[0], w_down[0]

        pos_a, pos_b, d_pack = route(expert_a, slot_a, expert_b, slot_b, gate_b, dy_b, num_experts, seg)
        pos_col_a, pos_col_b = pos_a.reshape(tokens, 1), pos_b.reshape(tokens, 1)

        def move(rows):
            return lax.all_to_all(rows.reshape(group_size, seg, hidden), 'ep', 0, 0, tiled=True).reshape(group_size * seg, hidden)

        d_out_b = move(d_pack)
        h_b, pack_b, *saved_b = attn_forward(x_b, w_q, w_k, w_v, w_o, gain_attn, gain_moe, pos_b, True, num_experts, seg)
        recv_b = move(pack_b)
        h_a, pack_a = attn_forward(x_a, w_q, w_k, w_v, w_o, gain_attn, gain_moe, pos_a, False, num_experts, seg)
        recv_a = move(pack_a)

        n_b, ids_b = active_blocks(recv_b, half)
        d_in_b, u_c, d_c, act_b, d_zg, d_zu = ffn_backward(n_b, ids_b, recv_b, d_out_b, w_gate, w_up, w_down, half)
        d_back = move(d_in_b)
        n_a, ids_a = active_blocks(recv_a, half)
        o_a = ffn_forward(n_a, ids_a, recv_a, w_gate, w_up, w_down, half)
        back_a = move(o_a)
        d_wgate, d_wup, d_wdown = ffn_grads(n_b, u_c, d_c, act_b, d_zg, d_zu, 2 * half)

        d_x, attn_grads = attn_backward(num_experts, x_b, h_b, dy_b, saved_b, d_back, pos_col_b, w_q, w_k, w_v, w_o, gain_attn, gain_moe)
        attn_grads = group_sum(attn_grads)
        y_a = combine(num_experts, h_a, back_a, pos_col_a, gate_a)
        return (y_a, d_x, attn_grads[0], attn_grads[1], attn_grads[2], attn_grads[3], d_wgate[None], d_wup[None], d_wdown[None])

    return jax.shard_map(device_program, mesh=mesh, in_specs=(row_spec, row_spec, row_spec, rep_two, rep_two, rep_two, rep_two, rep_one, rep_one, expert_spec, expert_spec, expert_spec, row_spec, row_spec, row_spec, row_spec, row_spec, row_spec), out_specs=(row_spec, row_spec, grad_spec, grad_spec, grad_spec, grad_spec, expert_grad_spec, expert_grad_spec, expert_grad_spec), check_vma=False)
```

time: 1320 us -> 716 us (0.54)
  the two profiles are of different devices: /device:TPU:0 before, /device:TPU:3 now
where the time goes in v1:
time: 716 us
  Pallas kernels  496 us (69%)
  waiting for transfers between devices  163 us (23%)
  starting transfers between devices  31.9 us (4%)
  local copies, waits for them, and re-layouts  13.4 us (2%)
  other arithmetic  11.2 us (2%)
    pallas_call x1, Pallas kernels, group_sum(): pl.pallas_call(reduce_kernel, in_specs=[pl.BlockSpec(memory_space=pltpu.V...  171 us
    all_to_all x5, waiting for transfers between devices, move(): lax.all_to_all(rows.reshape(group_size, seg, hidden), 'ep', 0, 0, tiled=T...  163 us
    pallas_call x1, Pallas kernels, ffn_backward(): pl.pallas_call(functools.partial(ffn_bwd_kernel, half, chunk), grid_spec=...  96.6 us
    pallas_call x1, Pallas kernels, ffn_forward(): pl.pallas_call(functools.partial(ffn_fwd_kernel, half, chunk), grid_spec=...  59.6 us
    pallas_call x1, Pallas kernels, ffn_grads(): pl.pallas_call(ffn_grad_kernel, grid_spec=pltpu.PrefetchScalarGridSpec(nu...  57.7 us
    pallas_call x2, Pallas kernels, attn_forward(): pl.pallas_call(functools.partial(attn_kernel, seg), grid=(seqs,), in_spec...  45.5 us
    pallas_call x1, Pallas kernels, attn_backward(): pl.pallas_call(functools.partial(attn_bwd_kernel, num_experts), grid=(tok...  44.6 us
    all_to_all x5, starting transfers between devices, move(): lax.all_to_all(rows.reshape(group_size, seg, hidden), 'ep', 0, 0, tiled=T...  31.9 us
  transfers between devices with their start and end apart: 5, of which 3 were waited for; matrix products, arithmetic and copies ran while one was open for 2% of the time, Pallas kernels for 66%

profile of v1, /device:TPU:3, one launch (start us, length us, event | category | flops | bytes accessed | tf_op | source)
XLA Modules:
  0.0 716.4 jit_solution(16066906151662213010)
XLA Ops:
  0.6 1.6 copy.33.gate_ref
  2.2 10.6 %route.1 = (s32[1,1024]{1,0:T(1,128)}, s32[1,1024]{1,0:T(1,128)}, bf16[3072,768]{1,0:T(8,128)(2,1)}) custom-call(s32[1,1024]{1,0:T(1,128)} %bitcast.38, s32[1,1024]{1,0:T(1,128)} %bitcast.39, s32[1,1024]{1,0:T(1,128)} %bitcast.40, s32[1,1024]{1,0:T(1,128)} %bitcast.41, bf16[1024,1]{1,0:T(8,128)(2,1)} %copy.33.gate_ref, bf16[1024,768]{1,0:T(8,128)(2,1)} %dy_ref.3), custom_call_target="tpu_custom_call" | custom-call | flops 3221225472 | bytes 3145728 | tf_op jit(solution)/shard_map/route/pallas_call | solution.py:98
  12.8 5.7 all-to-all-start.3
  19.7 23.0 %attn_fwd_keep.1 = (bf16[1024,768]{1,0:T(8,128)(2,1)}, bf16[3072,768]{1,0:T(8,128)(2,1)}, bf16[1024,768]{1,0:T(8,128)(2,1)}, bf16[1024,768]{1,0:T(8,128)(2,1)}, ...) custom-call(bf16[1024,768]{1,0:T(8,128)(2,1)} %x_ref.5, bf16[768,768]{1,0:T(8,128)(2,1)} %wq_ref.5, ...), custom_call_target="tpu_custom_call" | custom-call | flops 8455716864 | bytes 15728640 | tf_op jit(solution)/shard_map/attn_fwd_keep/pallas_call | solution.py:157
  42.7 79.7 %all-to-all-done.3 = bf16[8,384,768]{2,1,0:T(8,128)(2,1)} async-done(((bf16[8,384,768]{2,1,0:T(8,128)(2,1)}), bf16[8,384,768]{2,1,0:T(8,128)(2,1)}, u32[]{:S(2)}, u32[]{:S(2)}) %all-to-all-start.3) | async-done | bytes 4718624 | tf_op jit(solution)/shard_map/all_to_all | solution.py:641
  122.4 5.6 all-to-all-start.2
  128.0 22.5 %attn_fwd.1 = (bf16[1024,768]{1,0:T(8,128)(2,1)}, bf16[3072,768]{1,0:T(8,128)(2,1)}) custom-call(bf16[1024,768]{1,0:T(8,128)(2,1)} %x_ref.3, bf16[768,768]{1,0:T(8,128)(2,1)} %wq_ref.5, bf16[768,768]{1,0:T(8,128)(2,1)} %wk_ref.5, bf16[768,768]{1,0:T(8,128)(2,1)} %wv_ref.5, bf16[768,768]{1,0:T(8,128)(2,1)} %wo_ref.5, f32[1,768]{1,0:T(1,128)} %broadcast_in_dim.75.ga_ref, ...), custom_call_target="tpu_custom_call" | custom-call | flops 8455716864 | bytes 15728640 | tf_op jit(solution)/shard_map/attn_fwd/pallas_call | solution.py:157
  150.5 81.5 %all-to-all-done.2 = bf16[8,384,768]{2,1,0:T(8,128)(2,1)} async-done(((bf16[8,384,768]{2,1,0:T(8,128)(2,1)}), bf16[8,384,768]{2,1,0:T(8,128)(2,1)}, u32[]{:S(2)}, u32[]{:S(2)}) %all-to-all-start.2) | async-done | bytes 4718624 | tf_op jit(solution)/shard_map/all_to_all | solution.py:641
  232.0 5.6 all-to-all-start
  237.5 3.4 compare_reduce_fusion
  243.2 96.6 %ffn_bwd.1 = (bf16[3072,768]{1,0:T(8,128)(2,1)}, bf16[3072,768]{1,0:T(8,128)(2,1)}, bf16[3072,768]{1,0:T(8,128)(2,1)}, bf16[3072,3072]{1,0:T(8,128)(2,1)}, bf16[...) custom-call(s32[1]{0:T(128)} %bitcast.14.n_ref, s32[24]{0:T(128)} %select_reduce_fusion.ids_ref, ...), custom_call_target="tpu_custom_call" | custom-call | flops 43486543872 | bytes 42467328 | tf_op jit(solution)/shard_map/ffn_bwd/pallas_call | solution.py:311
  339.8 1.7 all-to-all-done
  341.5 10.6 %all-to-all-start.4 = ((bf16[8,384,768]{2,1,0:T(8,128)(2,1)}), bf16[8,384,768]{2,1,0:T(8,128)(2,1)}, u32[]{:S(2)}, u32[]{:S(2)}) async-start(bf16[8,384,768]{2,1,0:T(8,128)(2,1)} %bitcast.25), calls=%async_computation.4 | async-start | bytes 9437184 | tf_op jit(solution)/shard_map/all_to_all | solution.py:641
  355.0 3.4 compare_reduce_fusion.1
  360.6 59.6 %ffn_fwd.1 = bf16[3072,768]{1,0:T(8,128)(2,1)} custom-call(s32[1]{0:T(128)} %bitcast.5.n_ref, s32[24]{0:T(128)} %select_reduce_fusion.3.ids_ref, bf16[3072,768]{1,0:T(8,128)(2,1)} %bitcast.6.u0_ref.u1_ref, bf16[3072,768]{1,0:T(8,128)(2,1)} %bitcast.6.u0_ref.u1_ref, bf16[768,3072]{1,0:T(8,128)(2,1)} %bitcast.33, bf16[768,3072]{1,0:T(8,128)(2,1)} %bitcast.35, ...), custom_call_target="tpu_custom_call" | custom-call | flops 21743271936 | bytes 14155776 | tf_op jit(solution)/shard_map/ffn_fwd/pallas_call | solution.py:256
  420.2 57.7 %ffn_grads.1 = (f32[768,3072]{1,0:T(8,128)}, f32[768,3072]{1,0:T(8,128)}, f32[3072,768]{1,0:T(8,128)}) custom-call(s32[1]{0:T(128)} %bitcast.14.n_ref, bf16[3072,768]{1,0:T(8,128)(2,1)} %get-tuple-element.53.u_ref, bf16[3072,768]{1,0:T(8,128)(2,1)} %get-tuple-element.54.d_ref, bf16[3072,3072]{1,0:T(8,128)(2,1)} %get-tuple-element.55.act_ref, ...), custom_call_target="tpu_custom_call" | custom-call | flops 21743271936 | bytes 56623104 | tf_op jit(solution)/shard_map/ffn_grads/pallas_call | solution.py:350
  478.0 4.5 all-to-all-start.1
  482.5 44.6 %attn_bwd.1 = (bf16[1024,768]{1,0:T(8,128)(2,1)}, f32[4,768,768]{2,1,0:T(8,128)}) custom-call(bf16[1024,768]{1,0:T(8,128)(2,1)} %x_ref.5, bf16[1024,768]{1,0:T(8,128)(2,1)} %get-tuple-element.39.h_ref, bf16[1024,768]{1,0:T(8,128)(2,1)} %dy_ref.3, bf16[1024,768]{1,0:T(8,128)(2,1)} %get-tuple-element.40.q_ref, bf16[1024,768]{1,0:T(8,128)(2,1)} %get-tuple-element.41.k_ref, ...), custom_call_target="tpu_custom_call" | custom-call | flops 15703474176 | bytes 31457280 | tf_op jit(solution)/shard_map/attn_bwd/pallas_call | solution.py:402
  527.1 170.6 %group_sum.1 = (f32[768,768]{1,0:T(8,128)}, f32[768,768]{1,0:T(8,128)}, f32[768,768]{1,0:T(8,128)}, f32[768,768]{1,0:T(8,128)}) custom-call(f32[3072,768]{1,0:T(8,128)} %bitcast.45), custom_call_target="tpu_custom_call" | custom-call | flops 99999997952 | bytes 18874368 | tf_op jit(solution)/shard_map/group_sum/pallas_call | solution.py:609
  697.8 11.0 %combine.1 = bf16[1024,768]{1,0:T(8,128)(2,1)} custom-call(bf16[1024,768]{1,0:T(8,128)(2,1)} %get-tuple-element.36.h_ref, bf16[3072,768]{1,0:T(8,128)(2,1)} %bitcast.11.back_ref, s32[1024,1]{1,0:T(8,128)} %copy.34.pos_ref, bf16[1024,1]{1,0:T(8,128)(2,1)} %copy.35.gate_ref), custom_call_target="tpu_custom_call" | custom-call | flops 1610612736 | bytes 4718592 | tf_op jit(solution)/shard_map/combine/pallas_call | solution.py:425
  708.8 3.4 copy.41
  712.1 1.4 copy.42
  713.6 1.4 copy.43
  715.0 1.4 copy.44
  (37 shorter events, 8.5 us)
Async XLA Ops:
  12.8 5.7 copy-start.6
  12.8 6.3 copy-start.7
  12.8 109.6 %all-to-all-start.3 = ((bf16[8,384,768]{2,1,0:T(8,128)(2,1)}), bf16[8,384,768]{2,1,0:T(8,128)(2,1)}, u32[]{:S(2)}, u32[]{:S(2)}) async-start(bf16[8,384,768]{2,1,0:T(8,128)(2,1)} %bitcast.29), calls=%async_computation.3 | async-start | bytes 9437184 | tf_op jit(solution)/shard_map/all_to_all | solution.py:641
  122.4 109.5 %all-to-all-start.2 = ((bf16[8,384,768]{2,1,0:T(8,128)(2,1)}), bf16[8,384,768]{2,1,0:T(8,128)(2,1)}, u32[]{:S(2)}, u32[]{:S(2)}) async-start(bf16[8,384,768]{2,1,0:T(8,128)(2,1)} %bitcast.28), calls=%async_computation.2 | async-start | bytes 9437184 | tf_op jit(solution)/shard_map/all_to_all | solution.py:641
  232.0 109.5 %all-to-all-start = ((bf16[8,384,768]{2,1,0:T(8,128)(2,1)}), bf16[8,384,768]{2,1,0:T(8,128)(2,1)}, u32[]{:S(2)}, u32[]{:S(2)}) async-start(bf16[8,384,768]{2,1,0:T(8,128)(2,1)} %bitcast.26), calls=%async_computation | async-start | bytes 9437184 | tf_op jit(solution)/shard_map/all_to_all | solution.py:641
  341.5 10.6 %copy-start.3 = (bf16[1024,1]{0,1:T(2,128)(2,1)S(1)}, bf16[1024,1]{0,1:T(2,128)(2,1)}, u32[]{:S(2)}) copy-start(bf16[1024,1]{0,1:T(2,128)(2,1)} %param.32) | copy-start | bytes 6148
  341.5 11.4 %copy-start.5 = (s32[1,1024]{1,0:T(1,128)S(1)}, s32[1,1024]{1,0:T(1,128)}, u32[]{:S(2)}) copy-start(s32[1,1024]{1,0:T(1,128)} %get-tuple-element.38.pos_ref) | copy-start | bytes 12292
  341.5 12.5 %copy-start.4 = (s32[1,1024]{1,0:T(1,128)S(1)}, s32[1,1024]{1,0:T(1,128)}, u32[]{:S(2)}) copy-start(s32[1,1024]{1,0:T(1,128)} %get-tuple-element.35.pos_ref) | copy-start | bytes 12292
  341.5 136.4 %all-to-all-start.4 = ((bf16[8,384,768]{2,1,0:T(8,128)(2,1)}), bf16[8,384,768]{2,1,0:T(8,128)(2,1)}, u32[]{:S(2)}, u32[]{:S(2)}) async-start(bf16[8,384,768]{2,1,0:T(8,128)(2,1)} %bitcast.25), calls=%async_computation.4 | async-start | bytes 9437184 | tf_op jit(solution)/shard_map/all_to_all | solution.py:641
  478.0 219.8 %all-to-all-start.1 = ((bf16[8,384,768]{2,1,0:T(8,128)(2,1)}), bf16[8,384,768]{2,1,0:T(8,128)(2,1)}, u32[]{:S(2)}, u32[]{:S(2)}) async-start(bf16[8,384,768]{2,1,0:T(8,128)(2,1)} %bitcast.27), calls=%async_computation.1 | async-start | bytes 9437184 | tf_op jit(solution)/shard_map/all_to_all | solution.py:641
  697.8 14.4 %copy-start.2 = (f32[768,768]{1,0:T(8,128)S(1)}, f32[768,768]{1,0:T(8,128)}, u32[]{:S(2)}) copy-start(f32[768,768]{1,0:T(8,128)} %get-tuple-element.81) | copy-start | bytes 7077892
  708.8 4.8 copy-start.1
  712.1 2.8 copy-start

commit v2 on v1

--- a/solution.py
+++ b/solution.py
@@ -84,27 +84,6 @@
     return pos
 
 
-def route_kernel(num_experts, ea_ref, sa_ref, eb_ref, sb_ref, gate_ref, dy_ref, pos_a_ref, pos_b_ref, d_pack_ref, scaled):
-    seg = d_pack_ref.shape[0] // num_experts
-    route_one(ea_ref, sa_ref, pos_a_ref, num_experts, seg)
-    pos_b = route_one(eb_ref, sb_ref, pos_b_ref, num_experts, seg)
-    scaled[...] = (dy_ref[...].astype(F32) * gate_ref[...].astype(F32)).astype(BF)
-    pack_rows(pos_b, scaled, d_pack_ref, seg)
-
-
-def route(expert_a, slot_a, expert_b, slot_b, gate_b, dy_b, num_experts, seg):
-    tokens, hidden = dy_b.shape
-    row = jax.ShapeDtypeStruct((1, tokens), jnp.int32)
-    return pl.pallas_call(
-        functools.partial(route_kernel, num_experts),
-        out_shape=(row, row, jax.ShapeDtypeStruct((num_experts * seg, hidden), BF)),
-        scratch_shapes=[pltpu.VMEM((tokens, hidden), BF)],
-        compiler_params=pltpu.CompilerParams(vmem_limit_bytes=VMEM_LIMIT),
-        cost_estimate=pl.CostEstimate(flops=4 * tokens * tokens * hidden, bytes_accessed=2 * 2 * tokens * hidden, transcendentals=0),
-        name='route',
-    )(expert_a.reshape(1, tokens), slot_a.reshape(1, tokens), expert_b.reshape(1, tokens), slot_b.reshape(1, tokens), gate_b, dy_b)
-
-
 def softmax_head(q_head, k_head, causal):
     scores = jnp.where(causal, mm_nt(q_head, k_head) * HEAD_DIM ** -0.5, -1e30)
     expd = jnp.exp(scores - jnp.max(scores, axis=-1, keepdims=True))
@@ -115,8 +94,8 @@
     return lax.broadcasted_iota(jnp.int32, (seq_len, seq_len), 0) >= lax.broadcasted_iota(jnp.int32, (seq_len, seq_len), 1)
 
 
-def attn_kernel(chunk, x_ref, wq_ref, wk_ref, wv_ref, wo_ref, ga_ref, gm_ref, pos_ref, h_ref, pack_ref, *rest):
-    q_ref, k_ref, v_ref, mixed_ref, u_all = rest
+def attn_rows(x_ref, w_refs, ga_ref, gm_ref, h_ref, q_ref, k_ref, v_ref, mixed_ref, u_all, seq):
+    wq_ref, wk_ref, wv_ref, wo_ref = w_refs
     seq_len, hidden = x_ref.shape
     x_f = x_ref[...].astype(F32)
     normed = norm_rows(x_f, ga_ref[...])
@@ -130,41 +109,119 @@
         mixed_ref[:, cols] = mm(probs, v_ref[:, cols]).astype(BF)
     h_rows = (x_f + mm(mixed_ref[...], wo_ref[...])).astype(BF)
     h_ref[...] = h_rows
+    u_all[pl.ds(pl.multiple_of(seq * seq_len, seq_len), seq_len), :] = norm_rows(h_rows.astype(F32), gm_ref[...])
+
+
+def head_kernel(group, ea_ref, sa_ref, eb_ref, sb_ref, gate_ref, dy_ref, xa_ref, xb_ref, wq_ref, wk_ref, wv_ref, wo_ref, ga_ref, gm_ref,
+                pos_a_ref, pos_b_ref, ha_ref, pack_a_ref, hb_ref, q_ref, k_ref, v_ref, mixed_ref, recv_d_ref, recv_u_ref,
+                rows_all, pack_d, pack_u, qa, ka, va, ma, send_d, got_d, send_u, got_u, own):
     step = pl.program_id(0)
-    u_all[pl.ds(pl.multiple_of(step * seq_len, seq_len), seq_len), :] = norm_rows(h_rows.astype(F32), gm_ref[...])
-
-    @pl.when(step == pl.num_programs(0) - 1)
-    def _():
-        pack_rows(pos_ref[...], u_all, pack_ref, chunk)
-
-
-def attn_forward(x_rows, w_q, w_k, w_v, w_o, gain_attn, gain_moe, pos_row, keep, num_experts, seg):
-    tokens, hidden = x_rows.shape
+    seqs = pl.num_programs(0) // 2
+    me = lax.axis_index('ep')
+    seg = pack_d.shape[0] // group
+    w_refs = (wq_ref, wk_ref, wv_ref, wo_ref)
+
+    def rows_of(index):
+        return pl.ds(pl.multiple_of(index * seg, seg), seg)
+
+    def out_copy(packed, landing, send_sem, recv_sem, shift):
+        to = lax.rem(me + shift, group)
+        return pltpu.make_async_remote_copy(
+            src_ref=packed.at[rows_of(to), :], dst_ref=landing.at[rows_of(me), :], send_sem=send_sem.at[shift - 1], recv_sem=recv_sem.at[shift - 1],
+            device_id={'ep': to}, device_id_type=pl.DeviceIdType.MESH)
+
+    def own_copy(packed, landing, which):
+        return pltpu.make_async_copy(packed.at[rows_of(me), :], landing.at[rows_of(me), :], own.at[which])
+
+    def pack_and_send(pos_row, packed, landing, send_sem, recv_sem, which):
+        tokens = pos_row.shape[1]
+
+        def pack_for(to):
+            want = to * seg + lax.broadcasted_iota(jnp.int32, (seg, tokens), 0)
+            onehot = jnp.where(want == pos_row, 1.0, 0.0).astype(BF)
+            packed[rows_of(to), :] = mm(onehot, rows_all[...]).astype(BF)
+
+        def body(shift, carry):
+            pack_for(lax.rem(me + shift, group))
+            out_copy(packed, landing, send_sem, recv_sem, shift).start()
+            return carry
+
+        lax.fori_loop(1, group, body, 0)
+        pack_for(me)
+        own_copy(packed, landing, which).start()
+
+    def finish(packed, landing, send_sem, recv_sem, which):
+        def body(shift, carry):
+            copy = out_copy(packed, landing, send_sem, recv_sem, shift)
+            copy.wait_recv()
+            copy.wait_send()
+            return carry
+
+        lax.fori_loop(1, group, body, 0)
+        own_copy(packed, landing, which).wait()
+
+    @pl.when(step == 0)
+    def _():
+        barrier = pltpu.get_barrier_semaphore()
+
+        def greet(shift, carry):
+            pl.semaphore_signal(barrier, inc=1, device_id={'ep': lax.rem(me + shift, group)}, device_id_type=pl.DeviceIdType.MESH)
+            return carry
+
+        lax.fori_loop(1, group, greet, 0)
+        pos_b = route_one(eb_ref, sb_ref, pos_b_ref, group, seg)
+        rows_all[...] = (dy_ref[...].astype(F32) * gate_ref[...].astype(F32)).astype(BF)
+        pl.semaphore_wait(barrier, group - 1)
+        pack_and_send(pos_b, pack_d, recv_d_ref, send_d, got_d, 0)
+
+    @pl.when(step < seqs)
+    def _():
+        attn_rows(xb_ref, w_refs, ga_ref, gm_ref, hb_ref, q_ref, k_ref, v_ref, mixed_ref, rows_all, step)
+
+    @pl.when(step == seqs - 1)
+    def _():
+        pack_and_send(pos_b_ref[...], pack_u, recv_u_ref, send_u, got_u, 1)
+
+    @pl.when(step >= seqs)
+    def _():
+        attn_rows(xa_ref, w_refs, ga_ref, gm_ref, ha_ref, qa, ka, va, ma, rows_all, step - seqs)
+
+    @pl.when(step == 2 * seqs - 1)
+    def _():
+        pos_a = route_one(ea_ref, sa_ref, pos_a_ref, group, seg)
+        pack_rows(pos_a, rows_all, pack_a_ref, seg)
+        finish(pack_d, recv_d_ref, send_d, got_d, 0)
+        finish(pack_u, recv_u_ref, send_u, got_u, 1)
+
+
+def head(x_a, x_b, dy_b, gate_b, tables, weights, gain_attn, gain_moe, group, seg):
+    tokens, hidden = x_a.shape
     seq_len = min(tokens, SEQ_MAX)
     seqs = tokens // seq_len
-    rows = pl.BlockSpec((seq_len, hidden), lambda i: (i, 0))
-    whole = pl.BlockSpec((hidden, hidden), lambda i: (0, 0))
-    gain = pl.BlockSpec((1, hidden), lambda i: (0, 0))
+    rows_b = pl.BlockSpec((seq_len, hidden), lambda i: (jnp.minimum(i, seqs - 1), 0))
+    rows_a = pl.BlockSpec((seq_len, hidden), lambda i: (jnp.maximum(i - seqs, 0), 0))
+    once = pl.Buffered(1)
+
+    def fixed(*shape):
+        return pl.BlockSpec(shape, lambda i: (0,) * len(shape), pipeline_mode=once)
+
+    row = jax.ShapeDtypeStruct((1, tokens), jnp.int32)
+    row_out = pl.BlockSpec((1, tokens), lambda i: (0, 0))
     full = jax.ShapeDtypeStruct((tokens, hidden), BF)
-    out_shape = [full, jax.ShapeDtypeStruct((num_experts * seg, hidden), BF)]
-    out_specs = [rows, pl.BlockSpec((num_experts * seg, hidden), lambda i: (0, 0))]
-    scratch = [pltpu.VMEM((tokens, hidden), BF)]
-    if keep:
-        out_shape += [full] * 4
-        out_specs += [rows] * 4
-    else:
-        scratch = [pltpu.VMEM((seq_len, hidden), BF)] * 4 + scratch
+    slots = jax.ShapeDtypeStruct((group * seg, hidden), BF)
+    dma = pltpu.SemaphoreType.DMA((group - 1,))
     return pl.pallas_call(
-        functools.partial(attn_kernel, seg),
-        grid=(seqs,),
-        in_specs=[rows, whole, whole, whole, whole, gain, gain, pl.BlockSpec((1, tokens), lambda i: (0, 0))],
-        out_specs=out_specs,
-        out_shape=out_shape,
-        scratch_shapes=scratch,
-        compiler_params=pltpu.CompilerParams(vmem_limit_bytes=VMEM_LIMIT, dimension_semantics=('arbitrary',)),
-        cost_estimate=pl.CostEstimate(flops=14 * tokens * hidden * hidden, bytes_accessed=20 * tokens * hidden, transcendentals=tokens * seq_len * 6),
-        name='attn_fwd_keep' if keep else 'attn_fwd',
-    )(x_rows, w_q, w_k, w_v, w_o, gain_attn[None, :], gain_moe[None, :], pos_row)
+        functools.partial(head_kernel, group),
+        grid=(2 * seqs,),
+        in_specs=[fixed(1, tokens)] * 4 + [fixed(tokens, 1), fixed(tokens, hidden), rows_a, rows_b] + [fixed(hidden, hidden)] * 4 + [fixed(1, hidden)] * 2,
+        out_specs=[row_out, row_out, rows_a, pl.BlockSpec((group * seg, hidden), lambda i: (0, 0))] + [rows_b] * 5 + [pl.BlockSpec(memory_space=pl.ANY)] * 2,
+        out_shape=[row, row, full, slots] + [full] * 5 + [slots, slots],
+        scratch_shapes=[pltpu.VMEM((tokens, hidden), BF), pltpu.VMEM((group * seg, hidden), BF), pltpu.VMEM((group * seg, hidden), BF)]
+        + [pltpu.VMEM((seq_len, hidden), BF)] * 4 + [dma] * 4 + [pltpu.SemaphoreType.DMA((2,))],
+        compiler_params=pltpu.CompilerParams(vmem_limit_bytes=VMEM_LIMIT, dimension_semantics=('arbitrary',), collective_id=1, has_side_effects=True),
+        cost_estimate=pl.CostEstimate(flops=10 ** 11, bytes_accessed=60 * tokens * hidden, transcendentals=0),
+        name='head',
+    )(*[table.reshape(1, tokens) for table in tables], gate_b, dy_b, x_a, x_b, *weights, gain_attn[None, :], gain_moe[None, :])
 
 
 def weight_specs(hidden, ff):
@@ -634,18 +691,14 @@
         half = seg // 3
         w_gate, w_up, w_down = w_gate[0], w_up[0], w_down[0]
 
-        pos_a, pos_b, d_pack = route(expert_a, slot_a, expert_b, slot_b, gate_b, dy_b, num_experts, seg)
-        pos_col_a, pos_col_b = pos_a.reshape(tokens, 1), pos_b.reshape(tokens, 1)
-
         def move(rows):
             return lax.all_to_all(rows.reshape(group_size, seg, hidden), 'ep', 0, 0, tiled=True).reshape(group_size * seg, hidden)
 
-        d_out_b = move(d_pack)
-        h_b, pack_b, *saved_b = attn_forward(x_b, w_q, w_k, w_v, w_o, gain_attn, gain_moe, pos_b, True, num_experts, seg)
-        recv_b = move(pack_b)
-        h_a, pack_a = attn_forward(x_a, w_q, w_k, w_v, w_o, gain_attn, gain_moe, pos_a, False, num_experts, seg)
+        tables = (expert_a, slot_a, expert_b, slot_b)
+        pos_a, pos_b, h_a, pack_a, h_b, *rest = head(x_a, x_b, dy_b, gate_b, tables, (w_q, w_k, w_v, w_o), gain_attn, gain_moe, group_size, seg)
+        *saved_b, d_out_b, recv_b = rest
+        pos_col_a, pos_col_b = pos_a.reshape(tokens, 1), pos_b.reshape(tokens, 1)
         recv_a = move(pack_a)
-
         n_b, ids_b = active_blocks(recv_b, half)
         d_in_b, u_c, d_c, act_b, d_zg, d_zu = ffn_backward(n_b, ids_b, recv_b, d_out_b, w_gate, w_up, w_down, half)
         d_back = move(d_in_b)

time: 716 us -> 694 us (0.969)
  the two profiles are of different devices: /device:TPU:3 before, /device:TPU:0 now
where the time goes in v2:
time: 694 us; the launch traced here: 692 us
  Pallas kernels  538 us (78%)
  waiting for transfers between devices  64.5 us (9%)
  starting transfers between devices  61 us (9%)
  local copies, waits for them, and re-layouts  16 us (2%)
  other arithmetic  11.2 us (2%)
    pallas_call x1, Pallas kernels, head(): pl.pallas_call(functools.partial(head_kernel, group), grid=(2 * seqs,), i...  178 us
    pallas_call x1, Pallas kernels, group_sum(): pl.pallas_call(reduce_kernel, in_specs=[pl.BlockSpec(memory_space=pltpu.V...  174 us
    all_to_all x3, waiting for transfers between devices, move(): lax.all_to_all(rows.reshape(group_size, seg, hidden), 'ep', 0, 0, tiled=T...  64.5 us
    all_to_all x3, starting transfers between devices, move(): lax.all_to_all(rows.reshape(group_size, seg, hidden), 'ep', 0, 0, tiled=T...  61 us
    pallas_call x1, Pallas kernels, ffn_backward(): pl.pallas_call(functools.partial(ffn_bwd_kernel, half, chunk), grid_spec=...  51.1 us
    pallas_call x1, Pallas kernels, attn_backward(): pl.pallas_call(functools.partial(attn_bwd_kernel, num_experts), grid=(tok...  44.6 us
    pallas_call x1, Pallas kernels, ffn_forward(): pl.pallas_call(functools.partial(ffn_fwd_kernel, half, chunk), grid_spec=...  43.9 us
    pallas_call x1, Pallas kernels, ffn_grads(): pl.pallas_call(ffn_grad_kernel, grid_spec=pltpu.PrefetchScalarGridSpec(nu...  36.2 us
  transfers between devices with their start and end apart: 3, of which 2 were waited for; matrix products, arithmetic and copies ran while one was open for 2% of the time, Pallas kernels for 51%

profile of v2, /device:TPU:0, one launch (start us, length us, event | category | flops | bytes accessed | tf_op | source)
XLA Modules:
  0.0 691.9 jit_solution(7395538996396458910)
XLA Ops:
  0.6 1.3 broadcast_in_dim.73.ga_ref
  1.9 1.3 broadcast_in_dim.74.gm_ref
  3.2 1.6 copy.33.gate_ref
  4.7 178.1 %head.1 = (s32[1,1024]{1,0:T(1,128)}, s32[1,1024]{1,0:T(1,128)}, bf16[1024,768]{1,0:T(8,128)(2,1)}, bf16[3072,768]{1,0:T(8,128)(2,1)}, bf16[1024,768]{1,0:T(8,12...) custom-call(s32[1,1024]{1,0:T(1,128)} %bitcast.34, ...), custom_call_target="tpu_custom_call" | custom-call | flops 99999997952 | bytes 47185920 | tf_op jit(solution)/shard_map/head/pallas_call | solution.py:213
  182.8 41.6 %all-to-all-start = ((bf16[8,384,768]{2,1,0:T(8,128)(2,1)}), bf16[8,384,768]{2,1,0:T(8,128)(2,1)}, u32[]{:S(2)}, u32[]{:S(2)}) async-start(bf16[8,384,768]{2,1,0:T(8,128)(2,1)} %bitcast.24), calls=%async_computation | async-start | bytes 9437184 | tf_op jit(solution)/shard_map/all_to_all | solution.py:695
  224.4 3.4 compare_reduce_fusion
  229.9 51.1 %ffn_bwd.1 = (bf16[3072,768]{1,0:T(8,128)(2,1)}, bf16[3072,768]{1,0:T(8,128)(2,1)}, bf16[3072,768]{1,0:T(8,128)(2,1)}, bf16[3072,3072]{1,0:T(8,128)(2,1)}, bf16[...) custom-call(s32[1]{0:T(128)} %bitcast.14.n_ref, s32[24]{0:T(128)} %select_reduce_fusion.ids_ref, ...), custom_call_target="tpu_custom_call" | custom-call | flops 43486543872 | bytes 42467328 | tf_op jit(solution)/shard_map/ffn_bwd/pallas_call | solution.py:368
  281.0 48.3 %all-to-all-done = bf16[8,384,768]{2,1,0:T(8,128)(2,1)} async-done(((bf16[8,384,768]{2,1,0:T(8,128)(2,1)}), bf16[8,384,768]{2,1,0:T(8,128)(2,1)}, u32[]{:S(2)}, u32[]{:S(2)}) %all-to-all-start) | async-done | bytes 4718624 | tf_op jit(solution)/shard_map/all_to_all | solution.py:695
  329.4 4.9 all-to-all-start.2
  337.3 36.2 %ffn_grads.1 = (f32[768,3072]{1,0:T(8,128)}, f32[768,3072]{1,0:T(8,128)}, f32[3072,768]{1,0:T(8,128)}) custom-call(s32[1]{0:T(128)} %bitcast.14.n_ref, bf16[3072,768]{1,0:T(8,128)(2,1)} %get-tuple-element.53.u_ref, bf16[3072,768]{1,0:T(8,128)(2,1)} %get-tuple-element.54.d_ref, bf16[3072,3072]{1,0:T(8,128)(2,1)} %get-tuple-element.55.act_ref, ...), custom_call_target="tpu_custom_call" | custom-call | flops 21743271936 | bytes 56623104 | tf_op jit(solution)/shard_map/ffn_grads/pallas_call | solution.py:407
  373.5 3.4 compare_reduce_fusion.1
  379.2 43.9 %ffn_fwd.1 = bf16[3072,768]{1,0:T(8,128)(2,1)} custom-call(s32[1]{0:T(128)} %bitcast.5.n_ref, s32[24]{0:T(128)} %select_reduce_fusion.3.ids_ref, bf16[3072,768]{1,0:T(8,128)(2,1)} %bitcast.6.u0_ref.u1_ref, bf16[3072,768]{1,0:T(8,128)(2,1)} %bitcast.6.u0_ref.u1_ref, bf16[768,3072]{1,0:T(8,128)(2,1)} %bitcast.29, bf16[768,3072]{1,0:T(8,128)(2,1)} %bitcast.31, ...), custom_call_target="tpu_custom_call" | custom-call | flops 21743271936 | bytes 14155776 | tf_op jit(solution)/shard_map/ffn_fwd/pallas_call | solution.py:313
  423.1 16.2 %all-to-all-done.2 = bf16[8,384,768]{2,1,0:T(8,128)(2,1)} async-done(((bf16[8,384,768]{2,1,0:T(8,128)(2,1)}), bf16[8,384,768]{2,1,0:T(8,128)(2,1)}, u32[]{:S(2)}, u32[]{:S(2)}) %all-to-all-start.2) | async-done | bytes 4718624 | tf_op jit(solution)/shard_map/all_to_all | solution.py:695
  439.2 14.5 %all-to-all-start.1 = ((bf16[8,384,768]{2,1,0:T(8,128)(2,1)}), bf16[8,384,768]{2,1,0:T(8,128)(2,1)}, u32[]{:S(2)}, u32[]{:S(2)}) async-start(bf16[8,384,768]{2,1,0:T(8,128)(2,1)} %bitcast.25), calls=%async_computation.1 | async-start | bytes 9437184 | tf_op jit(solution)/shard_map/all_to_all | solution.py:695
  453.7 44.6 %attn_bwd.1 = (bf16[1024,768]{1,0:T(8,128)(2,1)}, f32[4,768,768]{2,1,0:T(8,128)}) custom-call(bf16[1024,768]{1,0:T(8,128)(2,1)} %x_ref.1, bf16[1024,768]{1,0:T(8,128)(2,1)} %get-tuple-element.38.h_ref, bf16[1024,768]{1,0:T(8,128)(2,1)} %dy_ref.3, bf16[1024,768]{1,0:T(8,128)(2,1)} %get-tuple-element.39.q_ref, bf16[1024,768]{1,0:T(8,128)(2,1)} %get-tuple-element.40.k_ref, ...), custom_call_target="tpu_custom_call" | custom-call | flops 15703474176 | bytes 31457280 | tf_op jit(solution)/shard_map/attn_bwd/pallas_call | solution.py:459
  498.4 173.6 %group_sum.1 = (f32[768,768]{1,0:T(8,128)}, f32[768,768]{1,0:T(8,128)}, f32[768,768]{1,0:T(8,128)}, f32[768,768]{1,0:T(8,128)}) custom-call(f32[3072,768]{1,0:T(8,128)} %bitcast.41), custom_call_target="tpu_custom_call" | custom-call | flops 99999997952 | bytes 18874368 | tf_op jit(solution)/shard_map/group_sum/pallas_call | solution.py:666
  672.0 11.0 %combine.1 = bf16[1024,768]{1,0:T(8,128)(2,1)} custom-call(bf16[1024,768]{1,0:T(8,128)(2,1)} %get-tuple-element.35.h_ref, bf16[3072,768]{1,0:T(8,128)(2,1)} %bitcast.11.back_ref, s32[1024,1]{1,0:T(8,128)} %copy.34.pos_ref, bf16[1024,1]{1,0:T(8,128)(2,1)} %copy.35.gate_ref), custom_call_target="tpu_custom_call" | custom-call | flops 1610612736 | bytes 4718592 | tf_op jit(solution)/shard_map/combine/pallas_call | solution.py:482
  683.0 1.4 copy.41
  684.4 1.1 copy-done.2
  685.5 1.4 copy.42
  686.9 1.1 copy-done.1
  688.0 1.4 copy.43
  689.4 1.1 copy-done
  690.5 1.4 copy.44
  (28 shorter events, 7.3 us)
Async XLA Ops:
  182.8 146.6 %all-to-all-start = ((bf16[8,384,768]{2,1,0:T(8,128)(2,1)}), bf16[8,384,768]{2,1,0:T(8,128)(2,1)}, u32[]{:S(2)}, u32[]{:S(2)}) async-start(bf16[8,384,768]{2,1,0:T(8,128)(2,1)} %bitcast.24), calls=%async_computation | async-start | bytes 9437184 | tf_op jit(solution)/shard_map/all_to_all | solution.py:695
  329.4 4.9 copy-start.4
  329.4 5.8 copy-start.6
  329.4 6.9 copy-start.5
  329.4 109.8 %all-to-all-start.2 = ((bf16[8,384,768]{2,1,0:T(8,128)(2,1)}), bf16[8,384,768]{2,1,0:T(8,128)(2,1)}, u32[]{:S(2)}, u32[]{:S(2)}) async-start(bf16[8,384,768]{2,1,0:T(8,128)(2,1)} %bitcast.23), calls=%async_computation.2 | async-start | bytes 9437184 | tf_op jit(solution)/shard_map/all_to_all | solution.py:695
  439.2 232.7 %all-to-all-start.1 = ((bf16[8,384,768]{2,1,0:T(8,128)(2,1)}), bf16[8,384,768]{2,1,0:T(8,128)(2,1)}, u32[]{:S(2)}, u32[]{:S(2)}) async-start(bf16[8,384,768]{2,1,0:T(8,128)(2,1)} %bitcast.25), calls=%async_computation.1 | async-start | bytes 9437184 | tf_op jit(solution)/shard_map/all_to_all | solution.py:695
  672.0 11.0 %copy-start.3 = (f32[768,768]{1,0:T(8,128)S(1)}, f32[768,768]{1,0:T(8,128)}, u32[]{:S(2)}) copy-start(f32[768,768]{1,0:T(8,128)} %get-tuple-element.80) | copy-start | bytes 7077892
  683.0 2.5 copy-start.2
  685.5 2.5 copy-start.1
  688.0 2.5 copy-start

commit v3 on v2

--- a/solution.py
+++ b/solution.py
@@ -20,6 +20,22 @@
     return ((3 * tokens * choices // num_experts + 7) // 8) * 8
 
 
+def params(dims):
+    return pltpu.CompilerParams(vmem_limit_bytes=VMEM_LIMIT, dimension_semantics=('arbitrary',) * dims)
+
+
+def cost(flops, moved):
+    return pl.CostEstimate(flops=flops, bytes_accessed=moved, transcendentals=0)
+
+
+def one_where(condition):
+    return jnp.where(condition, 1.0, 0.0).astype(BF)
+
+
+def iota(shape, dim):
+    return lax.broadcasted_iota(jnp.int32, shape, dim)
+
+
 def mm(lhs, rhs):
     return jnp.dot(lhs, rhs, preferred_element_type=F32)
 
@@ -52,9 +68,9 @@
 
     def body(c, carry):
         base = pl.multiple_of(c * chunk, chunk)
-        want = base + lax.broadcasted_iota(jnp.int32, (chunk, tokens), 0)
-        onehot = jnp.where(want == pos_row, 1.0, 0.0).astype(BF)
-        dst_ref[pl.ds(base, chunk), :] = mm(onehot, src_ref[...]).astype(BF)
+        want = base + iota((chunk, tokens), 0)
+        onehot = one_where(want == pos_row)
+        dst_ref[pl.ds(base, chunk), :] = mm(onehot, src_ref[:]).astype(BF)
         return carry
 
     lax.fori_loop(0, dst_ref.shape[0] // chunk, body, 0)
@@ -64,24 +80,23 @@
     seg = back_ref.shape[0] // num_experts
     total = jnp.zeros((pos_col.shape[0], back_ref.shape[1]), F32)
     for e in range(num_experts):
-        want = e * seg + lax.broadcasted_iota(jnp.int32, (pos_col.shape[0], seg), 1)
-        total += mm(jnp.where(want == pos_col, 1.0, 0.0).astype(BF), back_ref[pl.ds(e * seg, seg), :])
+        want = e * seg + iota((pos_col.shape[0], seg), 1)
+        total += mm(one_where(want == pos_col), back_ref[pl.ds(e * seg, seg), :])
     return total
 
 
 def route_one(e_ref, s_ref, pos_ref, num_experts, seg):
     tokens = e_ref.shape[1]
-    expert = e_ref[...]
-    kept = s_ref[...] >= 0
-    lane_expert = lax.broadcasted_iota(jnp.int32, (num_experts, tokens), 0)
-    onehot_f = jnp.where((lane_expert == expert) & kept, 1.0, 0.0)
+    expert = e_ref[:]
+    kept = s_ref[:] >= 0
+    sub_expert = iota((num_experts, tokens), 0)
+    onehot_f = jnp.where((sub_expert == expert) & kept, 1.0, 0.0)
     onehot = onehot_f.astype(BF)
-    before = lax.broadcasted_iota(jnp.int32, (tokens, tokens), 0) < lax.broadcasted_iota(jnp.int32, (tokens, tokens), 1)
-    rank = mm(onehot, jnp.where(before, 1.0, 0.0).astype(BF))
+    before = iota((tokens, tokens), 0) < iota((tokens, tokens), 1)
+    rank = mm(onehot, one_where(before))
     pos = expert * seg + jnp.sum(onehot_f * rank, axis=0, keepdims=True).astype(jnp.int32)
-    pos = jnp.where(kept, pos, FAR)
-    pos_ref[...] = pos
-    return pos
+    pos_ref[:] = jnp.where(kept, pos, FAR)
+    return expert, kept, onehot_f, rank
 
 
 def softmax_head(q_head, k_head, causal):
@@ -91,74 +106,171 @@
 
 
 def causal_mask(seq_len):
-    return lax.broadcasted_iota(jnp.int32, (seq_len, seq_len), 0) >= lax.broadcasted_iota(jnp.int32, (seq_len, seq_len), 1)
+    return iota((seq_len, seq_len), 0) >= iota((seq_len, seq_len), 1)
 
 
 def attn_rows(x_ref, w_refs, ga_ref, gm_ref, h_ref, q_ref, k_ref, v_ref, mixed_ref, u_all, seq):
     wq_ref, wk_ref, wv_ref, wo_ref = w_refs
     seq_len, hidden = x_ref.shape
-    x_f = x_ref[...].astype(F32)
-    normed = norm_rows(x_f, ga_ref[...])
-    q_ref[...] = mm(normed, wq_ref[...]).astype(BF)
-    k_ref[...] = mm(normed, wk_ref[...]).astype(BF)
-    v_ref[...] = mm(normed, wv_ref[...]).astype(BF)
+    x_f = x_ref[:].astype(F32)
+    normed = norm_rows(x_f, ga_ref[:])
+    q_ref[:] = mm(normed, wq_ref[:]).astype(BF)
+    k_ref[:] = mm(normed, wk_ref[:]).astype(BF)
+    v_ref[:] = mm(normed, wv_ref[:]).astype(BF)
     causal = causal_mask(seq_len)
     for head in range(hidden // HEAD_DIM):
         cols = pl.ds(head * HEAD_DIM, HEAD_DIM)
         probs = softmax_head(q_ref[:, cols], k_ref[:, cols], causal).astype(BF)
         mixed_ref[:, cols] = mm(probs, v_ref[:, cols]).astype(BF)
-    h_rows = (x_f + mm(mixed_ref[...], wo_ref[...])).astype(BF)
-    h_ref[...] = h_rows
-    u_all[pl.ds(pl.multiple_of(seq * seq_len, seq_len), seq_len), :] = norm_rows(h_rows.astype(F32), gm_ref[...])
+    h_rows = (x_f + mm(mixed_ref[:], wo_ref[:])).astype(BF)
+    h_ref[:] = h_rows
+    u_all[pl.ds(pl.multiple_of(seq * seq_len, seq_len), seq_len), :] = norm_rows(h_rows.astype(F32), gm_ref[:])
+
+
+PIECES = 4
+SEND_ORDER = (1, 2, 3, 0)
 
 
 def head_kernel(group, ea_ref, sa_ref, eb_ref, sb_ref, gate_ref, dy_ref, xa_ref, xb_ref, wq_ref, wk_ref, wv_ref, wo_ref, ga_ref, gm_ref,
                 pos_a_ref, pos_b_ref, ha_ref, pack_a_ref, hb_ref, q_ref, k_ref, v_ref, mixed_ref, recv_d_ref, recv_u_ref,
-                rows_all, pack_d, pack_u, qa, ka, va, ma, send_d, got_d, send_u, got_u, own):
+                rows_all, pos_cross, meta, meta_in, qa, ka, va, ma, slot_rows, s_meta, r_meta, own, *buffers):
     step = pl.program_id(0)
     seqs = pl.num_programs(0) // 2
     me = lax.axis_index('ep')
-    seg = pack_d.shape[0] // group
+    core, chip = lax.rem(me, 2), me // 2
+    side = chip // 2
+    local = lax.rem(me, 4)
+    is_mid = (chip == 1) | (chip == 2)
+    is_end = jnp.logical_not(is_mid)
+    partner = 2 * chip + 1 - core
+    relay = 2 * (2 - side) + core
+    end_dev = 2 * (3 * side) + core
+    tokens = rows_all.shape[0]
+    seg = slot_rows.shape[0]
+    piece = tokens // PIECES
     w_refs = (wq_ref, wk_ref, wv_ref, wo_ref)
-
-    def rows_of(index):
-        return pl.ds(pl.multiple_of(index * seg, seg), seg)
-
-    def out_copy(packed, landing, send_sem, recv_sem, shift):
-        to = lax.rem(me + shift, group)
-        return pltpu.make_async_remote_copy(
-            src_ref=packed.at[rows_of(to), :], dst_ref=landing.at[rows_of(me), :], send_sem=send_sem.at[shift - 1], recv_sem=recv_sem.at[shift - 1],
-            device_id={'ep': to}, device_id_type=pl.DeviceIdType.MESH)
-
-    def own_copy(packed, landing, which):
-        return pltpu.make_async_copy(packed.at[rows_of(me), :], landing.at[rows_of(me), :], own.at[which])
-
-    def pack_and_send(pos_row, packed, landing, send_sem, recv_sem, which):
-        tokens = pos_row.shape[1]
-
-        def pack_for(to):
-            want = to * seg + lax.broadcasted_iota(jnp.int32, (seg, tokens), 0)
-            onehot = jnp.where(want == pos_row, 1.0, 0.0).astype(BF)
-            packed[rows_of(to), :] = mm(onehot, rows_all[...]).astype(BF)
-
-        def body(shift, carry):
-            pack_for(lax.rem(me + shift, group))
-            out_copy(packed, landing, send_sem, recv_sem, shift).start()
-            return carry
-
-        lax.fori_loop(1, group, body, 0)
-        pack_for(me)
-        own_copy(packed, landing, which).start()
-
-    def finish(packed, landing, send_sem, recv_sem, which):
-        def body(shift, carry):
-            copy = out_copy(packed, landing, send_sem, recv_sem, shift)
-            copy.wait_recv()
-            copy.wait_send()
-            return carry
-
-        lax.fori_loop(1, group, body, 0)
-        own_copy(packed, landing, which).wait()
+    tensors = (buffers[:10] + (recv_d_ref, 0), buffers[10:] + (recv_u_ref, 1))
+
+    def remote(src, dst, send_sem, recv_sem, to):
+        return pltpu.make_async_remote_copy(src_ref=src, dst_ref=dst, send_sem=send_sem, recv_sem=recv_sem, device_id={'ep': to}, device_id_type=pl.DeviceIdType.MESH)
+
+    def part(index, size):
+        return pl.ds(pl.multiple_of(index * size, size), size)
+
+    class Exchange:
+        def __init__(self, refs):
+            (self.near, self.cross, self.win, self.s_near, self.r_near, self.s_cross, self.r_cross, self.s_end, self.r_end, self.pair, self.recv, self.which) = refs
+            self.s_pair, self.r_pair = self.pair.at[0], self.pair.at[1]
+
+        def near_copy(self, shift):
+            to = lax.rem(local + shift, 4)
+            return remote(self.near.at[part(to, seg), :], self.recv.at[part(me, seg), :], self.s_near.at[shift - 1], self.r_near.at[shift - 1], 4 * side + to)
+
+        def self_copy(self):
+            return pltpu.make_async_copy(self.near.at[part(local, seg), :], self.recv.at[part(me, seg), :], own.at[self.which])
+
+        def cross_copy(self, a, j):
+            at = part(j, piece)
+            return remote(self.cross.at[at, :], self.win.at[2 * a + core, at, :], self.s_cross.at[j], self.r_cross.at[a * PIECES + j], relay)
+
+        def end_copy(self, a, j):
+            at = self.win.at[2 * a + core, pl.ds(j * piece, piece), :]
+            return remote(at, at, self.s_end.at[a * PIECES + j], self.r_end.at[a * PIECES + j], end_dev)
+
+        def pair_copy(self, a, j, whose):
+            at = self.win.at[2 * a + whose, pl.ds(j * piece, piece), :]
+            return remote(at, at, self.s_pair.at[a * PIECES + j], self.r_pair.at[a * PIECES + j], partner)
+
+        def pack_and_send(self, pos_row, cross_row):
+            def pack_for(row, base, size, dst):
+                want = base + iota((size, tokens), 0)
+                dst[:] = mm(one_where(want == row), rows_all[:]).astype(BF)
+
+            def cross_body(i, carry):
+                j = lax.rem(i + SEND_ORDER[0], PIECES)
+                pack_for(cross_row, j * piece, piece, self.cross.at[part(j, piece), :])
+                self.cross_copy(chip - 2 * side, j).start()
+                return carry
+
+            lax.fori_loop(0, PIECES, cross_body, 0)
+
+            def body(shift, carry):
+                to = lax.rem(local + shift, 4)
+                pack_for(pos_row, (4 * side + to) * seg, seg, self.near.at[part(to, seg), :])
+                self.near_copy(shift).start()
+                return carry
+
+            lax.fori_loop(1, 4, body, 0)
+            pack_for(pos_row, me * seg, seg, self.near.at[part(local, seg), :])
+            self.self_copy().start()
+
+        def forward(self, j):
+            @pl.when(is_mid)
+            def _():
+                for a in range(2):
+                    self.cross_copy(a, j).wait_recv()
+                    if j > 0:
+                        self.end_copy(a, j).start()
+                    if j < PIECES - 1:
+                        self.pair_copy(a, j, core).start()
+
+            if j > 0:
+                @pl.when(is_end)
+                def _():
+                    for a in range(2):
+                        self.end_copy(a, j).wait_recv()
+                        self.pair_copy(a, j, core).start()
+
+        def arrived(self):
+            for role, pieces in ((is_mid, range(PIECES - 1)), (is_end, range(1, PIECES))):
+                @pl.when(role)
+                def _(pieces=pieces):
+                    for a in range(2):
+                        for j in pieces:
+                            self.pair_copy(a, j, 1 - core).wait_recv()
+
+        def take(self):
+            base = jnp.where(is_mid, 0, piece)
+
+            def body(source, carry):
+                first = meta_in[source, pl.ds(me, 1), :][:, :1]
+                count = meta_in[source, pl.ds(group + me, 1), :][:, :1]
+                window = self.win[source, pl.ds(pl.multiple_of(base, piece), tokens - piece), :]
+                slot = iota((seg, tokens - piece), 0)
+                lane = base + iota((seg, tokens - piece), 1)
+                pick = one_where((lane == first + slot) & (slot < count))
+                slot_rows[:] = mm(pick, window).astype(BF)
+                flush = pltpu.make_async_copy(slot_rows, self.recv.at[part(4 * (1 - side) + source, seg), :], own.at[self.which])
+                flush.start()
+                flush.wait()
+                return carry
+
+            lax.fori_loop(0, 4, body, 0)
+
+        def finish(self):
+            for shift in range(1, 4):
+                self.near_copy(shift).wait_recv()
+                self.near_copy(shift).wait_send()
+            for j in range(PIECES):
+                self.cross_copy(chip - 2 * side, j).wait_send()
+            for role, pieces in ((is_mid, range(PIECES - 1)), (is_end, range(1, PIECES))):
+                @pl.when(role)
+                def _(pieces=pieces):
+                    for a in range(2):
+                        for j in pieces:
+                            self.pair_copy(a, j, core).wait_send()
+
+            @pl.when(is_mid)
+            def _():
+                for a in range(2):
+                    for j in range(1, PIECES):
+                        self.end_copy(a, j).wait_send()
+
+    exch_d, exch_u = Exchange(tensors[0]), Exchange(tensors[1])
+
+    def meta_copy(shift):
+        to = 4 * (1 - side) + lax.rem(local + shift, 4)
+        return remote(meta, meta_in.at[local], s_meta.at[shift], r_meta.at[shift], to)
 
     @pl.when(step == 0)
     def _():
@@ -169,10 +281,25 @@
             return carry
 
         lax.fori_loop(1, group, greet, 0)
-        pos_b = route_one(eb_ref, sb_ref, pos_b_ref, group, seg)
-        rows_all[...] = (dy_ref[...].astype(F32) * gate_ref[...].astype(F32)).astype(BF)
+        expert, kept, onehot_f, rank = route_one(eb_ref, sb_ref, pos_b_ref, group, seg)
+        row_e = iota((group, group), 0)
+        col_e = iota((group, group), 1)
+        row_mid = (row_e >= 2) & (row_e < 6)
+        same_chip = (row_e // 2) == (col_e // 2)
+        reach = jnp.where(same_chip & ((row_mid & (col_e < row_e)) | (jnp.logical_not(row_mid) & (col_e >= row_e))), 1.0, 0.0).astype(BF)
+        reached = jnp.sum(mm(reach, onehot_f.astype(BF)), axis=1, keepdims=True)
+        one_e = iota((group, 1), 0)
+        start = jnp.where((one_e >= 2) & (one_e < 6), reached, tokens - reached)
+        count = jnp.sum(onehot_f, axis=1, keepdims=True)
+        meta[pl.ds(0, group), :] = jnp.broadcast_to(start.astype(jnp.int32), (group, 128))
+        meta[pl.ds(group, group), :] = jnp.broadcast_to(count.astype(jnp.int32), (group, 128))
+        at = jnp.sum(onehot_f * (start + rank), axis=0, keepdims=True).astype(jnp.int32)
+        pos_cross[:] = jnp.where(kept & ((expert // 4) != side), at, FAR)
+        rows_all[:] = (dy_ref[:].astype(F32) * gate_ref[:].astype(F32)).astype(BF)
         pl.semaphore_wait(barrier, group - 1)
-        pack_and_send(pos_b, pack_d, recv_d_ref, send_d, got_d, 0)
+        for shift in range(4):
+            meta_copy(shift).start()
+        exch_d.pack_and_send(pos_b_ref[:], pos_cross[:])
 
     @pl.when(step < seqs)
     def _():
@@ -180,7 +307,12 @@
 
     @pl.when(step == seqs - 1)
     def _():
-        pack_and_send(pos_b_ref[...], pack_u, recv_u_ref, send_u, got_u, 1)
+        exch_u.pack_and_send(pos_b_ref[:], pos_cross[:])
+
+    for late, j in enumerate(SEND_ORDER):
+        @pl.when(step == seqs - 1 + late)
+        def _(j=j):
+            exch_d.forward(j)
 
     @pl.when(step >= seqs)
     def _():
@@ -188,10 +320,22 @@
 
     @pl.when(step == 2 * seqs - 1)
     def _():
-        pos_a = route_one(ea_ref, sa_ref, pos_a_ref, group, seg)
-        pack_rows(pos_a, rows_all, pack_a_ref, seg)
-        finish(pack_d, recv_d_ref, send_d, got_d, 0)
-        finish(pack_u, recv_u_ref, send_u, got_u, 1)
+        route_one(ea_ref, sa_ref, pos_a_ref, group, seg)
+        pack_rows(pos_a_ref[:], rows_all, pack_a_ref, seg)
+        exch_u.forward(SEND_ORDER[0])
+        for shift in range(4):
+            meta_copy(shift).wait_recv()
+            meta_copy(shift).wait_send()
+        exch_d.self_copy().wait()
+        exch_u.self_copy().wait()
+        exch_d.arrived()
+        exch_d.take()
+        for j in SEND_ORDER[1:]:
+            exch_u.forward(j)
+        exch_u.arrived()
+        exch_u.take()
+        exch_d.finish()
+        exch_u.finish()
 
 
 def head(x_a, x_b, dy_b, gate_b, tables, weights, gain_attn, gain_moe, group, seg):
@@ -205,21 +349,26 @@
     def fixed(*shape):
         return pl.BlockSpec(shape, lambda i: (0,) * len(shape), pipeline_mode=once)
 
+    def dma(*shape):
+        return pltpu.SemaphoreType.DMA(shape)
+
     row = jax.ShapeDtypeStruct((1, tokens), jnp.int32)
     row_out = pl.BlockSpec((1, tokens), lambda i: (0, 0))
     full = jax.ShapeDtypeStruct((tokens, hidden), BF)
     slots = jax.ShapeDtypeStruct((group * seg, hidden), BF)
-    dma = pltpu.SemaphoreType.DMA((group - 1,))
+    exchange = [pltpu.VMEM((4 * seg, hidden), BF), pltpu.VMEM((tokens, hidden), BF), pltpu.VMEM((4, tokens, hidden), BF)]
+    exchange += [dma(3), dma(3), dma(PIECES), dma(2 * PIECES), dma(2 * PIECES), dma(2 * PIECES), dma(2, 2 * PIECES)]
+    scratch = [pltpu.VMEM((tokens, hidden), BF), pltpu.VMEM((1, tokens), jnp.int32), pltpu.VMEM((2 * group, 128), jnp.int32), pltpu.VMEM((4, 2 * group, 128), jnp.int32)]
+    scratch += [pltpu.VMEM((seq_len, hidden), BF)] * 4 + [pltpu.VMEM((seg, hidden), BF), dma(4), dma(4), dma(2)]
     return pl.pallas_call(
         functools.partial(head_kernel, group),
         grid=(2 * seqs,),
         in_specs=[fixed(1, tokens)] * 4 + [fixed(tokens, 1), fixed(tokens, hidden), rows_a, rows_b] + [fixed(hidden, hidden)] * 4 + [fixed(1, hidden)] * 2,
         out_specs=[row_out, row_out, rows_a, pl.BlockSpec((group * seg, hidden), lambda i: (0, 0))] + [rows_b] * 5 + [pl.BlockSpec(memory_space=pl.ANY)] * 2,
         out_shape=[row, row, full, slots] + [full] * 5 + [slots, slots],
-        scratch_shapes=[pltpu.VMEM((tokens, hidden), BF), pltpu.VMEM((group * seg, hidden), BF), pltpu.VMEM((group * seg, hidden), BF)]
-        + [pltpu.VMEM((seq_len, hidden), BF)] * 4 + [dma] * 4 + [pltpu.SemaphoreType.DMA((2,))],
+        scratch_shapes=scratch + exchange + exchange,
         compiler_params=pltpu.CompilerParams(vmem_limit_bytes=VMEM_LIMIT, dimension_semantics=('arbitrary',), collective_id=1, has_side_effects=True),
-        cost_estimate=pl.CostEstimate(flops=10 ** 11, bytes_accessed=60 * tokens * hidden, transcendentals=0),
+        cost_estimate=cost(10 ** 11, 60 * tokens * hidden),
         name='head',
     )(*[table.reshape(1, tokens) for table in tables], gate_b, dy_b, x_a, x_b, *weights, gain_attn[None, :], gain_moe[None, :])
 
@@ -238,8 +387,8 @@
 
 
 def join_pair(first_ref, second_ref, both):
-    second = second_ref[...]
-    return jnp.concatenate([first_ref[...], jnp.where(both, second, jnp.zeros_like(second))], axis=0)
+    second = second_ref[:]
+    return jnp.concatenate([first_ref[:], jnp.where(both, second, jnp.zeros_like(second))], axis=0)
 
 
 def pair_loop(n_ref, ids_ref, buf, out_ref, sem, half, compute):
@@ -273,7 +422,7 @@
 
     @pl.when(2 * step >= n_ref[0])
     def _():
-        dst[...] = jnp.zeros_like(dst)
+        dst[:] = jnp.zeros_like(dst)
 
     for copy in copies(step):
         copy.start()
@@ -287,18 +436,18 @@
 def ffn_fwd_kernel(half, chunk, n_ref, ids_ref, u0_ref, u1_ref, wg_ref, wu_ref, wd_ref, o_ref, acc, buf, sem):
     def compute(both, dst):
         u_rows = join_pair(u0_ref, u1_ref, both)
-        acc[...] = jnp.zeros_like(acc)
+        acc[:] = jnp.zeros_like(acc)
 
         def body(c, carry):
             cols = pl.ds(pl.multiple_of(c * chunk, chunk), chunk)
             z_gate = mm(u_rows, wg_ref[:, cols])
             z_up = mm(u_rows, wu_ref[:, cols])
             act = (z_gate * jax.nn.sigmoid(z_gate) * z_up).astype(BF)
-            acc[...] += mm(act, wd_ref[cols, :])
+            acc[:] += mm(act, wd_ref[cols, :])
             return carry
 
-        lax.fori_loop(0, wg_ref.shape[1] // chunk, body, 0)
-        dst[...] = acc[...].astype(BF)
+        lax.fori_loop(0, wg_ref.shape[1] // chunk, body, 0, unroll=2)
+        dst[:] = acc[:].astype(BF)
 
     pair_loop(n_ref, ids_ref, buf, o_ref, sem, half, compute)
 
@@ -320,8 +469,8 @@
             scratch_shapes=pair_scratch(half, hidden),
         ),
         out_shape=jax.ShapeDtypeStruct((rows, hidden), BF),
-        compiler_params=pltpu.CompilerParams(vmem_limit_bytes=VMEM_LIMIT, dimension_semantics=('arbitrary',)),
-        cost_estimate=pl.CostEstimate(flops=3 * rows * hidden * ff, bytes_accessed=6 * hidden * ff, transcendentals=0),
+        compiler_params=params(1),
+        cost_estimate=cost(3 * rows * hidden * ff, 6 * hidden * ff),
         name='ffn_fwd',
     )(n_blocks, ids, u_rows, u_rows, w_gate, w_up, w_down)
 
@@ -330,9 +479,9 @@
     def compute(both, dst):
         u_rows = join_pair(u0_ref, u1_ref, both)
         d_out = join_pair(d0_ref, d1_ref, both)
-        uc_ref[...] = u_rows
-        dc_ref[...] = d_out
-        acc[...] = jnp.zeros_like(acc)
+        uc_ref[:] = u_rows
+        dc_ref[:] = d_out
+        acc[:] = jnp.zeros_like(acc)
 
         def body(c, carry):
             cols = pl.ds(pl.multiple_of(c * chunk, chunk), chunk)
@@ -346,11 +495,11 @@
             d_zu = (d_act * silu).astype(BF)
             dzg_ref[:, cols] = d_zg
             dzu_ref[:, cols] = d_zu
-            acc[...] += mm_nt(d_zg, wg_ref[:, cols]) + mm_nt(d_zu, wu_ref[:, cols])
+            acc[:] += mm_nt(d_zg, wg_ref[:, cols]) + mm_nt(d_zu, wu_ref[:, cols])
             return carry
 
         lax.fori_loop(0, wg_ref.shape[1] // chunk, body, 0)
-        dst[...] = acc[...].astype(BF)
+        dst[:] = acc[:].astype(BF)
 
     pair_loop(n_ref, ids_ref, buf, din_ref, sem, half, compute)
 
@@ -375,55 +524,70 @@
             scratch_shapes=pair_scratch(half, hidden),
         ),
         out_shape=(thin, thin, thin, wide, wide, wide),
-        compiler_params=pltpu.CompilerParams(vmem_limit_bytes=VMEM_LIMIT, dimension_semantics=('arbitrary',)),
-        cost_estimate=pl.CostEstimate(flops=6 * rows * hidden * ff, bytes_accessed=6 * hidden * ff + 3 * rows * ff, transcendentals=0),
+        compiler_params=params(1),
+        cost_estimate=cost(6 * rows * hidden * ff, 6 * hidden * ff + 3 * rows * ff),
         name='ffn_bwd',
     )(n_blocks, ids, u_rows, u_rows, d_out, d_out, w_gate, w_up, w_down)
 
 
-def ffn_grad_kernel(n_ref, u_ref, d_ref, act_ref, dzg_ref, dzu_ref, dwg_ref, dwu_ref, dwd_ref):
+def ffn_grad_kernel(half, n_ref, u_ref, d_ref, act_ref, dzg_ref, dzu_ref, dwg_ref, dwu_ref, dwd_ref):
     step = pl.program_id(1)
+    block = u_ref.shape[0]
+    held = (n_ref[0] + 1) // 2 * (2 * half) - step * block
 
     @pl.when(step == 0)
     def _():
-        dwg_ref[...] = jnp.zeros_like(dwg_ref)
-        dwu_ref[...] = jnp.zeros_like(dwu_ref)
-        dwd_ref[...] = jnp.zeros_like(dwd_ref)
-
-    @pl.when(2 * step < n_ref[0])
-    def _():
-        dwg_ref[...] += mm_tn(u_ref[...], dzg_ref[...])
-        dwu_ref[...] += mm_tn(u_ref[...], dzu_ref[...])
-        dwd_ref[...] += mm_tn(act_ref[...], d_ref[...])
-
-
-def ffn_grads(n_blocks, u_rows, d_out, act, d_zg, d_zu, block=256, chunk=1024):
+        for grad in (dwg_ref, dwu_ref, dwd_ref):
+            grad[:] = jnp.zeros_like(grad)
+
+    def add(size):
+        rows = pl.ds(0, size)
+        dwg_ref[:] += mm_tn(u_ref[rows, :], dzg_ref[rows, :])
+        dwu_ref[:] += mm_tn(u_ref[rows, :], dzu_ref[rows, :])
+        dwd_ref[:] += mm_tn(act_ref[rows, :], d_ref[rows, :])
+
+    @pl.when(held >= block)
+    def _():
+        add(block)
+
+    @pl.when((held > 0) & (held < block))
+    def _():
+        add(2 * half)
+
+
+def ffn_grads(n_blocks, u_rows, d_out, act, d_zg, d_zu, half, chunk=1024):
     rows, hidden = u_rows.shape
     ff = act.shape[1]
-    row_spec = pl.BlockSpec((block, hidden), lambda j, i, n: (step_index(n, i), 0))
-    wide_spec = pl.BlockSpec((block, chunk), lambda j, i, n: (step_index(n, i), j))
+    block = 4 * half
+
+    def last_held(n_ref, i):
+        return jnp.minimum(i, jnp.maximum((n_ref[0] + 3) // 4 - 1, 0))
+
+    row_spec = pl.BlockSpec((block, hidden), lambda j, i, n: (last_held(n, i), 0))
+    wide_spec = pl.BlockSpec((block, chunk), lambda j, i, n: (last_held(n, i), j))
     up_spec = pl.BlockSpec((hidden, chunk), lambda j, i, n: (0, j))
     down_spec = pl.BlockSpec((chunk, hidden), lambda j, i, n: (j, 0))
+    up = jax.ShapeDtypeStruct((hidden, ff), F32)
     return pl.pallas_call(
-        ffn_grad_kernel,
+        functools.partial(ffn_grad_kernel, half),
         grid_spec=pltpu.PrefetchScalarGridSpec(
             num_scalar_prefetch=1,
             grid=(ff // chunk, rows // block),
             in_specs=[row_spec, row_spec, wide_spec, wide_spec, wide_spec],
             out_specs=[up_spec, up_spec, down_spec],
         ),
-        out_shape=(jax.ShapeDtypeStruct((hidden, ff), F32), jax.ShapeDtypeStruct((hidden, ff), F32), jax.ShapeDtypeStruct((ff, hidden), F32)),
-        compiler_params=pltpu.CompilerParams(vmem_limit_bytes=VMEM_LIMIT, dimension_semantics=('arbitrary', 'arbitrary')),
-        cost_estimate=pl.CostEstimate(flops=3 * rows * hidden * ff, bytes_accessed=12 * hidden * ff + 3 * rows * ff, transcendentals=0),
+        out_shape=(up, up, jax.ShapeDtypeStruct((ff, hidden), F32)),
+        compiler_params=params(2),
+        cost_estimate=cost(3 * rows * hidden * ff, 12 * hidden * ff + 3 * rows * ff),
         name='ffn_grads',
     )(n_blocks, u_rows, d_out, act, d_zg, d_zu)
 
 
 def attn_bwd_kernel(num_experts, x_ref, h_ref, dy_ref, q_ref, k_ref, v_ref, mixed_ref, back_ref, pos_ref, wq_ref, wk_ref, wv_ref, wo_ref, ga_ref, gm_ref, dx_ref, dw_ref, dq, dk, dv, dmix):
     seq_len, hidden = x_ref.shape
-    d_u = unpack_rows(pos_ref[...], num_experts, back_ref).astype(BF)
-    d_h = (dy_ref[...].astype(F32) + norm_back(h_ref[...].astype(F32), gm_ref[...], d_u).astype(F32)).astype(BF)
-    dmix[...] = mm_nt(d_h, wo_ref[...]).astype(BF)
+    d_u = unpack_rows(pos_ref[:], num_experts, back_ref).astype(BF)
+    d_h = (dy_ref[:].astype(F32) + norm_back(h_ref[:].astype(F32), gm_ref[:], d_u).astype(F32)).astype(BF)
+    dmix[:] = mm_nt(d_h, wo_ref[:]).astype(BF)
     causal = causal_mask(seq_len)
     for head in range(hidden // HEAD_DIM):
         cols = pl.ds(head * HEAD_DIM, HEAD_DIM)
@@ -434,20 +598,20 @@
         d_scores = (probs * (d_probs - jnp.sum(d_probs * probs, axis=-1, keepdims=True)) * HEAD_DIM ** -0.5).astype(BF)
         dq[:, cols] = mm(d_scores, k_head).astype(BF)
         dk[:, cols] = mm_tn(d_scores, q_head).astype(BF)
-    x_f = x_ref[...].astype(F32)
-    normed = norm_rows(x_f, ga_ref[...])
+    x_f = x_ref[:].astype(F32)
+    normed = norm_rows(x_f, ga_ref[:])
 
     @pl.when(pl.program_id(0) == 0)
     def _():
-        dw_ref[...] = jnp.zeros_like(dw_ref)
+        dw_ref[:] = jnp.zeros_like(dw_ref)
 
     normed_t = normed.T
-    dw_ref[0] += mm(normed_t, dq[...])
-    dw_ref[1] += mm(normed_t, dk[...])
-    dw_ref[2] += mm(normed_t, dv[...])
-    dw_ref[3] += mm_tn(mixed_ref[...], d_h)
-    d_normed = (mm_nt(dq[...], wq_ref[...]) + mm_nt(dk[...], wk_ref[...]) + mm_nt(dv[...], wv_ref[...])).astype(BF)
-    dx_ref[...] = (d_h.astype(F32) + norm_back(x_f, ga_ref[...], d_normed).astype(F32)).astype(BF)
+    dw_ref[0] += mm(normed_t, dq[:])
+    dw_ref[1] += mm(normed_t, dk[:])
+    dw_ref[2] += mm(normed_t, dv[:])
+    dw_ref[3] += mm_tn(mixed_ref[:], d_h)
+    d_normed = (mm_nt(dq[:], wq_ref[:]) + mm_nt(dk[:], wk_ref[:]) + mm_nt(dv[:], wv_ref[:])).astype(BF)
+    dx_ref[:] = (d_h.astype(F32) + norm_back(x_f, ga_ref[:], d_normed).astype(F32)).astype(BF)
 
 
 def attn_backward(num_experts, x_rows, h_rows, dy_rows, saved, back, pos_col, w_q, w_k, w_v, w_o, gain_attn, gain_moe):
@@ -463,32 +627,45 @@
         out_specs=[rows, pl.BlockSpec((4, hidden, hidden), lambda i: (0, 0, 0))],
         out_shape=(jax.ShapeDtypeStruct((tokens, hidden), BF), jax.ShapeDtypeStruct((4, hidden, hidden), F32)),
         scratch_shapes=[pltpu.VMEM((seq_len, hidden), BF)] * 4,
-        compiler_params=pltpu.CompilerParams(vmem_limit_bytes=VMEM_LIMIT, dimension_semantics=('arbitrary',)),
-        cost_estimate=pl.CostEstimate(flops=26 * tokens * hidden * hidden, bytes_accessed=40 * tokens * hidden, transcendentals=tokens * seq_len * 6),
+        compiler_params=params(1),
+        cost_estimate=cost(26 * tokens * hidden * hidden, 40 * tokens * hidden),
         name='attn_bwd',
     )(x_rows, h_rows, dy_rows, *saved, back, pos_col, w_q, w_k, w_v, w_o, gain_attn[None, :], gain_moe[None, :])
 
 
-def combine_kernel(num_experts, h_ref, back_ref, pos_ref, gate_ref, y_ref):
-    picked = unpack_rows(pos_ref[...], num_experts, back_ref)
-    y_ref[...] = (h_ref[...].astype(F32) + gate_ref[...].astype(F32) * picked).astype(BF)
-
-
-def combine(num_experts, h_rows, back, pos_col, gate_col):
+def combine_kernel(num_experts, h_ref, back_ref, pos_ref, gate_ref, sum_ref, y_ref, *rest):
+    outs, sem = rest[:-1], rest[-1]
+    copies = [pltpu.make_async_copy(sum_ref, out, sem) for out in outs]
+
+    def when_mine(act):
+        for i, copy in enumerate(copies):
+            @pl.when(pl.program_id(0) == i)
+            def _(copy=copy):
+                act(copy)
+
+    when_mine(lambda copy: copy.start())
+    picked = unpack_rows(pos_ref[:], num_experts, back_ref)
+    y_ref[:] = (h_ref[:].astype(F32) + gate_ref[:].astype(F32) * picked).astype(BF)
+    when_mine(lambda copy: copy.wait())
+
+
+def combine(num_experts, h_rows, back, pos_col, gate_col, sums):
     tokens, hidden = h_rows.shape
-    block = min(tokens, 256)
+    count = sums.shape[0] // hidden
+    block = tokens // count
     rows = pl.BlockSpec((block, hidden), lambda i: (i, 0))
     one = pl.BlockSpec((block, 1), lambda i: (i, 0))
     return pl.pallas_call(
         functools.partial(combine_kernel, num_experts),
-        grid=(tokens // block,),
-        in_specs=[rows, pl.BlockSpec(back.shape, lambda i: (0, 0)), one, one],
-        out_specs=rows,
-        out_shape=jax.ShapeDtypeStruct((tokens, hidden), BF),
-        compiler_params=pltpu.CompilerParams(vmem_limit_bytes=VMEM_LIMIT, dimension_semantics=('arbitrary',)),
-        cost_estimate=pl.CostEstimate(flops=2 * tokens * tokens * hidden, bytes_accessed=6 * tokens * hidden, transcendentals=0),
+        grid=(count,),
+        in_specs=[rows, pl.BlockSpec(back.shape, lambda i: (0, 0)), one, one, pl.BlockSpec((hidden, hidden), lambda i: (i, 0))],
+        out_specs=[rows] + [pl.BlockSpec(memory_space=pl.ANY)] * count,
+        out_shape=[jax.ShapeDtypeStruct((tokens, hidden), BF)] + [jax.ShapeDtypeStruct((hidden, hidden), F32)] * count,
+        scratch_shapes=[pltpu.SemaphoreType.DMA],
+        compiler_params=params(1),
+        cost_estimate=cost(2 * tokens * tokens * hidden, 6 * tokens * hidden),
         name='combine',
-    )(h_rows, back, pos_col, gate_col)
+    )(h_rows, back, pos_col, gate_col, sums)
 
 
 def active_blocks(rows, half):
@@ -509,7 +686,7 @@
 
 
 def reduce_kernel(x_ref, *rest):
-    outs, (prt, acc, from_end, from_mid, tot, s_prt, r_prt, s_up, r_up, s_mid, r_mid, s_end, s_fwd, s_share, r_tot, r_share, s_out) = rest[:4], rest[4:]
+    out_ref, (prt, acc, from_end, from_mid, tot, s_prt, r_prt, s_up, r_up, s_mid, r_mid, s_end, s_fwd, s_share, r_tot, r_share, s_out) = rest[0], rest[1:]
     me = lax.axis_index('ep')
     core, z = lax.rem(me, 2), me // 2
     is_mid = (z == 1) | (z == 2)
@@ -649,12 +826,9 @@
         return carry
 
     lax.fori_loop(0, steps, finish, 0)
-    size = outs[0].shape[0]
-    flushes = [pltpu.make_async_copy(tot.at[pl.ds(i * size, size), :], out, s_out.at[i]) for i, out in enumerate(outs)]
-    for flush in flushes:
-        flush.start()
-    for flush in flushes:
-        flush.wait()
+    flush = pltpu.make_async_copy(tot, out_ref, s_out)
+    flush.start()
+    flush.wait()
 
 
 def group_sum(stacked):
@@ -666,11 +840,11 @@
     return pl.pallas_call(
         reduce_kernel,
         in_specs=[pl.BlockSpec(memory_space=pltpu.VMEM)],
-        out_specs=[pl.BlockSpec(memory_space=pl.ANY)] * count,
-        out_shape=[jax.ShapeDtypeStruct((size, hidden), F32)] * count,
-        scratch_shapes=[pltpu.VMEM((half, hidden), F32)] * 4 + [pltpu.VMEM((total, hidden), F32)] + [dma] * 11 + [pltpu.SemaphoreType.DMA((count,))],
+        out_specs=pl.BlockSpec(memory_space=pl.ANY),
+        out_shape=jax.ShapeDtypeStruct((total, hidden), F32),
+        scratch_shapes=[pltpu.VMEM((half, hidden), F32)] * 4 + [pltpu.VMEM((total, hidden), F32)] + [dma] * 11 + [pltpu.SemaphoreType.DMA],
         compiler_params=pltpu.CompilerParams(vmem_limit_bytes=VMEM_LIMIT, collective_id=0, has_side_effects=True),
-        cost_estimate=pl.CostEstimate(flops=10 ** 11, bytes_accessed=8 * total * hidden, transcendentals=0),
+        cost_estimate=cost(10 ** 11, 8 * total * hidden),
         name='group_sum',
     )(stacked.reshape(total, hidden))
 
@@ -705,11 +879,11 @@
         n_a, ids_a = active_blocks(recv_a, half)
         o_a = ffn_forward(n_a, ids_a, recv_a, w_gate, w_up, w_down, half)
         back_a = move(o_a)
-        d_wgate, d_wup, d_wdown = ffn_grads(n_b, u_c, d_c, act_b, d_zg, d_zu, 2 * half)
+        d_wgate, d_wup, d_wdown = ffn_grads(n_b, u_c, d_c, act_b, d_zg, d_zu, half)
 
         d_x, attn_grads = attn_backward(num_experts, x_b, h_b, dy_b, saved_b, d_back, pos_col_b, w_q, w_k, w_v, w_o, gain_attn, gain_moe)
         attn_grads = group_sum(attn_grads)
-        y_a = combine(num_experts, h_a, back_a, pos_col_a, gate_a)
-        return (y_a, d_x, attn_grads[0], attn_grads[1], attn_grads[2], attn_grads[3], d_wgate[None], d_wup[None], d_wdown[None])
+        y_a, *attn_grads = combine(num_experts, h_a, back_a, pos_col_a, gate_a, attn_grads)
+        return (y_a, d_x, *attn_grads, d_wgate[None], d_wup[None], d_wdown[None])
 
     return jax.shard_map(device_program, mesh=mesh, in_specs=(row_spec, row_spec, row_spec, rep_two, rep_two, rep_two, rep_two, rep_one, rep_one, expert_spec, expert_spec, expert_spec, row_spec, row_spec, row_spec, row_spec, row_spec, row_spec), out_specs=(row_spec, row_spec, grad_spec, grad_spec, grad_spec, grad_spec, expert_grad_spec, expert_grad_spec, expert_grad_spec), check_vma=False)

time: 694 us -> 658 us (0.948)
  starting transfers between devices: 61 us -> 22.9 us
  Pallas kernels: 538 us -> 567 us
  waiting for transfers between devices: 64.5 us -> 48.1 us
  local copies, waits for them, and re-layouts: 16 us -> 7.07 us
    all_to_all x3, starting transfers between devices: 61 us -> 22.9 us  [move(): lax.all_to_all(rows.reshape(group_size, seg, hidden), 'ep', 0, 0, tiled=T...]
    all_to_all x3, waiting for transfers between devices: 64.5 us -> 48.1 us  [move(): lax.all_to_all(rows.reshape(group_size, seg, hidden), 'ep', 0, 0, tiled=T...]
    pallas_call x1, Pallas kernels: 51.1 us -> 60.1 us  [ffn_backward(): pl.pallas_call(functools.partial(ffn_bwd_kernel, half, chunk), grid_spec=...]
    unnamed x20 -> x8, local copies, waits for them, and re-layouts: 11.4 us -> 2.45 us
    pallas_call x1, Pallas kernels: 178 us -> 187 us  [head(): pl.pallas_call(functools.partial(head_kernel, group), grid=(2 * seqs,), i...]
    pallas_call x2, Pallas kernels: 47.2 us -> 54.7 us  [the longest x1 42 us: ffn_grads(): pl.pallas_call(functools.partial(ffn_grad_kernel, half), grid_spec=pltpu....]
  transfers between devices with their start and end apart: 3 -> 3, of which waited for: 2 -> 2; matrix products, arithmetic and copies ran while one was open for 2% -> 2% of each run, Pallas kernels for 51% -> 56%
where the time goes in v3:
time: 658 us; the launch traced here: 657 us
  Pallas kernels  567 us (86%)
  waiting for transfers between devices  48.1 us (7%)
  starting transfers between devices  22.9 us (3%)
  other arithmetic  11.1 us (2%)
  local copies, waits for them, and re-layouts  7.07 us (1%)
    pallas_call x1, Pallas kernels, head(): pl.pallas_call(functools.partial(head_kernel, group), grid=(2 * seqs,), i...  187 us
    pallas_call x1, Pallas kernels, group_sum(): pl.pallas_call(reduce_kernel, in_specs=[pl.BlockSpec(memory_space=pltpu.V...  175 us
    pallas_call x1, Pallas kernels, ffn_backward(): pl.pallas_call(functools.partial(ffn_bwd_kernel, half, chunk), grid_spec=...  60.1 us
    all_to_all x3, waiting for transfers between devices, move(): lax.all_to_all(rows.reshape(group_size, seg, hidden), 'ep', 0, 0, tiled=T...  48.1 us
    pallas_call x1, Pallas kernels, ffn_forward(): pl.pallas_call(functools.partial(ffn_fwd_kernel, half, chunk), grid_spec=...  45.8 us
    pallas_call x1, Pallas kernels, attn_backward(): pl.pallas_call(functools.partial(attn_bwd_kernel, num_experts), grid=(tok...  44.6 us
    pallas_call x1, Pallas kernels, ffn_grads(): pl.pallas_call(functools.partial(ffn_grad_kernel, half), grid_spec=pltpu....  42 us
    all_to_all x3, starting transfers between devices, move(): lax.all_to_all(rows.reshape(group_size, seg, hidden), 'ep', 0, 0, tiled=T...  22.9 us
  transfers between devices with their start and end apart: 3, of which 2 were waited for; matrix products, arithmetic and copies ran while one was open for 2% of the time, Pallas kernels for 56%

profile of v3, /device:TPU:0, one launch (start us, length us, event | category | flops | bytes accessed | tf_op | source)
XLA Modules:
  0.0 657.1 jit_solution(5357115903718958497)
XLA Ops:
  0.6 1.3 broadcast_in_dim.73.ga_ref
  1.9 1.3 broadcast_in_dim.74.gm_ref
  3.2 1.6 copy.33.gate_ref
  4.7 186.9 %head.1 = (s32[1,1024]{1,0:T(1,128)}, s32[1,1024]{1,0:T(1,128)}, bf16[1024,768]{1,0:T(8,128)(2,1)}, bf16[3072,768]{1,0:T(8,128)(2,1)}, bf16[1024,768]{1,0:T(8,12...) custom-call(s32[1,1024]{1,0:T(1,128)} %bitcast.34, ...), custom_call_target="tpu_custom_call" | custom-call | flops 99999997952 | bytes 47185920 | tf_op jit(solution)/shard_map/head/pallas_call | solution.py:363
  191.7 5.0 all-to-all-start
  196.6 3.4 compare_reduce_fusion
  200.2 0.6 broadcast_subtract_fusion
  200.9 0.6 compare_select_fusion
  202.2 60.1 %ffn_bwd.1 = (bf16[3072,768]{1,0:T(8,128)(2,1)}, bf16[3072,768]{1,0:T(8,128)(2,1)}, bf16[3072,768]{1,0:T(8,128)(2,1)}, bf16[3072,3072]{1,0:T(8,128)(2,1)}, bf16[...) custom-call(s32[1]{0:T(128)} %bitcast.14.n_ref, s32[24]{0:T(128)} %select_reduce_fusion.ids_ref, ...), custom_call_target="tpu_custom_call" | custom-call | flops 43486543872 | bytes 42467328 | tf_op jit(solution)/shard_map/ffn_bwd/pallas_call | solution.py:517
  262.3 39.4 %all-to-all-done = bf16[8,384,768]{2,1,0:T(8,128)(2,1)} async-done(((bf16[8,384,768]{2,1,0:T(8,128)(2,1)}), bf16[8,384,768]{2,1,0:T(8,128)(2,1)}, u32[]{:S(2)}, u32[]{:S(2)}) %all-to-all-start) | async-done | bytes 4718624 | tf_op jit(solution)/shard_map/all_to_all | solution.py:869
  301.6 11.5 %all-to-all-start.2 = ((bf16[8,384,768]{2,1,0:T(8,128)(2,1)}), bf16[8,384,768]{2,1,0:T(8,128)(2,1)}, u32[]{:S(2)}, u32[]{:S(2)}) async-start(bf16[8,384,768]{2,1,0:T(8,128)(2,1)} %bitcast.23), calls=%async_computation.2 | async-start | bytes 9437184 | tf_op jit(solution)/shard_map/all_to_all | solution.py:869
  313.1 0.9 copy.36.gate_ref
  314.0 1.0 copy.35.pos_ref
  315.1 1.0 copy.34.pos_ref
  316.1 42.0 %ffn_grads.1 = (f32[768,3072]{1,0:T(8,128)}, f32[768,3072]{1,0:T(8,128)}, f32[3072,768]{1,0:T(8,128)}) custom-call(s32[1]{0:T(128)} %bitcast.14.n_ref, bf16[3072,768]{1,0:T(8,128)(2,1)} %get-tuple-element.55.u_ref, bf16[3072,768]{1,0:T(8,128)(2,1)} %get-tuple-element.56.d_ref, bf16[3072,3072]{1,0:T(8,128)(2,1)} %get-tuple-element.57.act_ref, ...), custom_call_target="tpu_custom_call" | custom-call | flops 21743271936 | bytes 56623104 | tf_op jit(solution)/shard_map/ffn_grads/pallas_call | solution.py:571
  358.1 3.4 compare_reduce_fusion.1
  361.6 0.6 broadcast_subtract_fusion.1
  362.4 0.6 compare_select_fusion.1
  363.7 45.8 %ffn_fwd.1 = bf16[3072,768]{1,0:T(8,128)(2,1)} custom-call(s32[1]{0:T(128)} %bitcast.5.n_ref, s32[24]{0:T(128)} %select_reduce_fusion.3.ids_ref, bf16[3072,768]{1,0:T(8,128)(2,1)} %bitcast.6.u0_ref.u1_ref, bf16[3072,768]{1,0:T(8,128)(2,1)} %bitcast.6.u0_ref.u1_ref, bf16[768,3072]{1,0:T(8,128)(2,1)} %bitcast.29, bf16[768,3072]{1,0:T(8,128)(2,1)} %bitcast.31, ...), custom_call_target="tpu_custom_call" | custom-call | flops 21743271936 | bytes 14155776 | tf_op jit(solution)/shard_map/ffn_fwd/pallas_call | solution.py:462
  409.4 8.7 %all-to-all-done.2 = bf16[8,384,768]{2,1,0:T(8,128)(2,1)} async-done(((bf16[8,384,768]{2,1,0:T(8,128)(2,1)}), bf16[8,384,768]{2,1,0:T(8,128)(2,1)}, u32[]{:S(2)}, u32[]{:S(2)}) %all-to-all-start.2) | async-done | bytes 4718624 | tf_op jit(solution)/shard_map/all_to_all | solution.py:869
  418.2 6.4 all-to-all-start.1
  424.6 44.6 %attn_bwd.1 = (bf16[1024,768]{1,0:T(8,128)(2,1)}, f32[4,768,768]{2,1,0:T(8,128)}) custom-call(bf16[1024,768]{1,0:T(8,128)(2,1)} %x_ref.1, bf16[1024,768]{1,0:T(8,128)(2,1)} %get-tuple-element.39.h_ref, bf16[1024,768]{1,0:T(8,128)(2,1)} %dy_ref.3, bf16[1024,768]{1,0:T(8,128)(2,1)} %get-tuple-element.40.q_ref, bf16[1024,768]{1,0:T(8,128)(2,1)} %get-tuple-element.41.k_ref, ...), custom_call_target="tpu_custom_call" | custom-call | flops 15703474176 | bytes 31457280 | tf_op jit(solution)/shard_map/attn_bwd/pallas_call | solution.py:623
  469.2 174.9 %group_sum.1.sum_ref = f32[3072,768]{1,0:T(8,128)} custom-call(f32[3072,768]{1,0:T(8,128)} %bitcast.41), custom_call_target="tpu_custom_call" | custom-call | flops 99999997952 | bytes 18874368 | tf_op jit(solution)/shard_map/group_sum/pallas_call | solution.py:840
  644.2 12.7 %combine.1 = (bf16[1024,768]{1,0:T(8,128)(2,1)}, f32[768,768]{1,0:T(8,128)}, f32[768,768]{1,0:T(8,128)}, f32[768,768]{1,0:T(8,128)}, f32[768,768]{1,0:T(8,128)}) custom-call(bf16[1024,768]{1,0:T(8,128)(2,1)} %get-tuple-element.36.h_ref, bf16[3072,768]{1,0:T(8,128)(2,1)} %bitcast.11.back_ref, s32[1024,1]{1,0:T(8,128)} %copy.35.pos_ref, ...), custom_call_target="tpu_custom_call" | custom-call | flops 1610612736 | bytes 4718592 | tf_op jit(solution)/shard_map/combine/pallas_call | solution.py:658
  (16 shorter events, 1.7 us)
Async XLA Ops:
  191.7 110.0 %all-to-all-start = ((bf16[8,384,768]{2,1,0:T(8,128)(2,1)}), bf16[8,384,768]{2,1,0:T(8,128)(2,1)}, u32[]{:S(2)}, u32[]{:S(2)}) async-start(bf16[8,384,768]{2,1,0:T(8,128)(2,1)} %bitcast.24), calls=%async_computation | async-start | bytes 9437184 | tf_op jit(solution)/shard_map/all_to_all | solution.py:869
  301.6 11.5 %copy-start = (bf16[1024,1]{0,1:T(2,128)(2,1)S(1)}, bf16[1024,1]{0,1:T(2,128)(2,1)}, u32[]{:S(2)}) copy-start(bf16[1024,1]{0,1:T(2,128)(2,1)} %param.32) | copy-start | bytes 6148
  301.6 12.4 %copy-start.2 = (s32[1,1024]{1,0:T(1,128)S(1)}, s32[1,1024]{1,0:T(1,128)}, u32[]{:S(2)}) copy-start(s32[1,1024]{1,0:T(1,128)} %get-tuple-element.38) | copy-start | bytes 12292
  301.6 13.4 %copy-start.1 = (s32[1,1024]{1,0:T(1,128)S(1)}, s32[1,1024]{1,0:T(1,128)}, u32[]{:S(2)}) copy-start(s32[1,1024]{1,0:T(1,128)} %get-tuple-element.47) | copy-start | bytes 12292
  301.6 116.5 %all-to-all-start.2 = ((bf16[8,384,768]{2,1,0:T(8,128)(2,1)}), bf16[8,384,768]{2,1,0:T(8,128)(2,1)}, u32[]{:S(2)}, u32[]{:S(2)}) async-start(bf16[8,384,768]{2,1,0:T(8,128)(2,1)} %bitcast.23), calls=%async_computation.2 | async-start | bytes 9437184 | tf_op jit(solution)/shard_map/all_to_all | solution.py:869
  418.2 226.0 %all-to-all-start.1 = ((bf16[8,384,768]{2,1,0:T(8,128)(2,1)}), bf16[8,384,768]{2,1,0:T(8,128)(2,1)}, u32[]{:S(2)}, u32[]{:S(2)}) async-start(bf16[8,384,768]{2,1,0:T(8,128)(2,1)} %bitcast.25), calls=%async_computation.1 | async-start | bytes 9437184 | tf_op jit(solution)/shard_map/all_to_all | solution.py:869

commit v4 on v3

--- a/solution.py
+++ b/solution.py
@@ -146,7 +146,7 @@
     relay = 2 * (2 - side) + core
     end_dev = 2 * (3 * side) + core
     tokens = rows_all.shape[0]
-    seg = slot_rows.shape[0]
+    seg = slot_rows.shape[1]
     piece = tokens // PIECES
     w_refs = (wq_ref, wk_ref, wv_ref, wo_ref)
     tensors = (buffers[:10] + (recv_d_ref, 0), buffers[10:] + (recv_u_ref, 1))
@@ -167,7 +167,10 @@
             return remote(self.near.at[part(to, seg), :], self.recv.at[part(me, seg), :], self.s_near.at[shift - 1], self.r_near.at[shift - 1], 4 * side + to)
 
         def self_copy(self):
-            return pltpu.make_async_copy(self.near.at[part(local, seg), :], self.recv.at[part(me, seg), :], own.at[self.which])
+            return pltpu.make_async_copy(self.near.at[part(local, seg), :], self.recv.at[part(me, seg), :], own.at[self.which, 4])
+
+        def flush(self, source):
+            return pltpu.make_async_copy(slot_rows.at[source], self.recv.at[part(4 * (1 - side) + source, seg), :], own.at[self.which, source])
 
         def cross_copy(self, a, j):
             at = part(j, piece)
@@ -239,13 +242,15 @@
                 slot = iota((seg, tokens - piece), 0)
                 lane = base + iota((seg, tokens - piece), 1)
                 pick = one_where((lane == first + slot) & (slot < count))
-                slot_rows[:] = mm(pick, window).astype(BF)
-                flush = pltpu.make_async_copy(slot_rows, self.recv.at[part(4 * (1 - side) + source, seg), :], own.at[self.which])
-                flush.start()
-                flush.wait()
+                slot_rows[source] = mm(pick, window).astype(BF)
+                self.flush(source).start()
                 return carry
 
             lax.fori_loop(0, 4, body, 0)
+
+        def flushed(self):
+            for source in range(4):
+                self.flush(source).wait()
 
         def finish(self):
             for shift in range(1, 4):
@@ -310,7 +315,7 @@
         exch_u.pack_and_send(pos_b_ref[:], pos_cross[:])
 
     for late, j in enumerate(SEND_ORDER):
-        @pl.when(step == seqs - 1 + late)
+        @pl.when(step == seqs - 2 + late)
         def _(j=j):
             exch_d.forward(j)
 
@@ -333,9 +338,11 @@
         for j in SEND_ORDER[1:]:
             exch_u.forward(j)
         exch_u.arrived()
+        exch_d.flushed()
         exch_u.take()
         exch_d.finish()
         exch_u.finish()
+        exch_u.flushed()
 
 
 def head(x_a, x_b, dy_b, gate_b, tables, weights, gain_attn, gain_moe, group, seg):
@@ -359,7 +366,7 @@
     exchange = [pltpu.VMEM((4 * seg, hidden), BF), pltpu.VMEM((tokens, hidden), BF), pltpu.VMEM((4, tokens, hidden), BF)]
     exchange += [dma(3), dma(3), dma(PIECES), dma(2 * PIECES), dma(2 * PIECES), dma(2 * PIECES), dma(2, 2 * PIECES)]
     scratch = [pltpu.VMEM((tokens, hidden), BF), pltpu.VMEM((1, tokens), jnp.int32), pltpu.VMEM((2 * group, 128), jnp.int32), pltpu.VMEM((4, 2 * group, 128), jnp.int32)]
-    scratch += [pltpu.VMEM((seq_len, hidden), BF)] * 4 + [pltpu.VMEM((seg, hidden), BF), dma(4), dma(4), dma(2)]
+    scratch += [pltpu.VMEM((seq_len, hidden), BF)] * 4 + [pltpu.VMEM((4, seg, hidden), BF), dma(4), dma(4), dma(2, 5)]
     return pl.pallas_call(
         functools.partial(head_kernel, group),
         grid=(2 * seqs,),

time: 658 us -> 664 us (level); the launches traced: 657 us -> 652 us
  no operation moved by 1% of the time
where the time goes in v4:
time: 664 us; the launch traced here: 652 us
  Pallas kernels  568 us (86%)
  waiting for transfers between devices  47.7 us (7%)
  starting transfers between devices  17.3 us (3%)
  other arithmetic  11.1 us (2%)
  local copies, waits for them, and re-layouts  7.07 us (1%)
    pallas_call x1, Pallas kernels, head(): pl.pallas_call(functools.partial(head_kernel, group), grid=(2 * seqs,), i...  189 us
    pallas_call x1, Pallas kernels, group_sum(): pl.pallas_call(reduce_kernel, in_specs=[pl.BlockSpec(memory_space=pltpu.V...  174 us
    pallas_call x1, Pallas kernels, ffn_backward(): pl.pallas_call(functools.partial(ffn_bwd_kernel, half, chunk), grid_spec=...  60.1 us
    all_to_all x3, waiting for transfers between devices, move(): lax.all_to_all(rows.reshape(group_size, seg, hidden), 'ep', 0, 0, tiled=T...  47.7 us
    pallas_call x1, Pallas kernels, ffn_forward(): pl.pallas_call(functools.partial(ffn_fwd_kernel, half, chunk), grid_spec=...  45.8 us
    pallas_call x1, Pallas kernels, attn_backward(): pl.pallas_call(functools.partial(attn_bwd_kernel, num_experts), grid=(tok...  44.6 us
    pallas_call x1, Pallas kernels, ffn_grads(): pl.pallas_call(functools.partial(ffn_grad_kernel, half), grid_spec=pltpu....  42 us
    all_to_all x3, starting transfers between devices, move(): lax.all_to_all(rows.reshape(group_size, seg, hidden), 'ep', 0, 0, tiled=T...  17.3 us
  transfers between devices with their start and end apart: 3, of which 2 were waited for; matrix products, arithmetic and copies ran while one was open for 2% of the time, Pallas kernels for 56%

profile of v4, /device:TPU:0, one launch (start us, length us, event | category | flops | bytes accessed | tf_op | source)
XLA Modules:
  0.0 651.6 jit_solution(10423575157665567312)
XLA Ops:
  0.6 1.3 broadcast_in_dim.73.ga_ref
  1.9 1.3 broadcast_in_dim.74.gm_ref
  3.2 1.6 copy.33.gate_ref
  4.7 188.8 %head.1 = (s32[1,1024]{1,0:T(1,128)}, s32[1,1024]{1,0:T(1,128)}, bf16[1024,768]{1,0:T(8,128)(2,1)}, bf16[3072,768]{1,0:T(8,128)(2,1)}, bf16[1024,768]{1,0:T(8,12...) custom-call(s32[1,1024]{1,0:T(1,128)} %bitcast.34, ...), custom_call_target="tpu_custom_call" | custom-call | flops 99999997952 | bytes 47185920 | tf_op jit(solution)/shard_map/head/pallas_call | solution.py:370
  193.5 4.8 all-to-all-start
  198.4 3.4 compare_reduce_fusion
  201.9 0.6 broadcast_subtract_fusion
  202.7 0.6 compare_select_fusion
  203.9 60.1 %ffn_bwd.1 = (bf16[3072,768]{1,0:T(8,128)(2,1)}, bf16[3072,768]{1,0:T(8,128)(2,1)}, bf16[3072,768]{1,0:T(8,128)(2,1)}, bf16[3072,3072]{1,0:T(8,128)(2,1)}, bf16[...) custom-call(s32[1]{0:T(128)} %bitcast.14.n_ref, s32[24]{0:T(128)} %select_reduce_fusion.ids_ref, ...), custom_call_target="tpu_custom_call" | custom-call | flops 43486543872 | bytes 42467328 | tf_op jit(solution)/shard_map/ffn_bwd/pallas_call | solution.py:524
  264.0 39.1 %all-to-all-done = bf16[8,384,768]{2,1,0:T(8,128)(2,1)} async-done(((bf16[8,384,768]{2,1,0:T(8,128)(2,1)}), bf16[8,384,768]{2,1,0:T(8,128)(2,1)}, u32[]{:S(2)}, u32[]{:S(2)}) %all-to-all-start) | async-done | bytes 4718624 | tf_op jit(solution)/shard_map/all_to_all | solution.py:876
  303.1 4.7 all-to-all-start.2
  307.9 0.9 copy.36.gate_ref
  308.8 1.0 copy.35.pos_ref
  309.8 1.0 copy.34.pos_ref
  310.8 42.0 %ffn_grads.1 = (f32[768,3072]{1,0:T(8,128)}, f32[768,3072]{1,0:T(8,128)}, f32[3072,768]{1,0:T(8,128)}) custom-call(s32[1]{0:T(128)} %bitcast.14.n_ref, bf16[3072,768]{1,0:T(8,128)(2,1)} %get-tuple-element.55.u_ref, bf16[3072,768]{1,0:T(8,128)(2,1)} %get-tuple-element.56.d_ref, bf16[3072,3072]{1,0:T(8,128)(2,1)} %get-tuple-element.57.act_ref, ...), custom_call_target="tpu_custom_call" | custom-call | flops 21743271936 | bytes 56623104 | tf_op jit(solution)/shard_map/ffn_grads/pallas_call | solution.py:578
  352.8 3.4 compare_reduce_fusion.1
  356.4 0.6 broadcast_subtract_fusion.1
  357.1 0.6 compare_select_fusion.1
  358.4 45.8 %ffn_fwd.1 = bf16[3072,768]{1,0:T(8,128)(2,1)} custom-call(s32[1]{0:T(128)} %bitcast.5.n_ref, s32[24]{0:T(128)} %select_reduce_fusion.3.ids_ref, bf16[3072,768]{1,0:T(8,128)(2,1)} %bitcast.6.u0_ref.u1_ref, bf16[3072,768]{1,0:T(8,128)(2,1)} %bitcast.6.u0_ref.u1_ref, bf16[768,3072]{1,0:T(8,128)(2,1)} %bitcast.29, bf16[768,3072]{1,0:T(8,128)(2,1)} %bitcast.31, ...), custom_call_target="tpu_custom_call" | custom-call | flops 21743271936 | bytes 14155776 | tf_op jit(solution)/shard_map/ffn_fwd/pallas_call | solution.py:469
  404.2 8.6 %all-to-all-done.2 = bf16[8,384,768]{2,1,0:T(8,128)(2,1)} async-done(((bf16[8,384,768]{2,1,0:T(8,128)(2,1)}), bf16[8,384,768]{2,1,0:T(8,128)(2,1)}, u32[]{:S(2)}, u32[]{:S(2)}) %all-to-all-start.2) | async-done | bytes 4718624 | tf_op jit(solution)/shard_map/all_to_all | solution.py:876
  412.8 7.7 %all-to-all-start.1 = ((bf16[8,384,768]{2,1,0:T(8,128)(2,1)}), bf16[8,384,768]{2,1,0:T(8,128)(2,1)}, u32[]{:S(2)}, u32[]{:S(2)}) async-start(bf16[8,384,768]{2,1,0:T(8,128)(2,1)} %bitcast.25), calls=%async_computation.1 | async-start | bytes 9437184 | tf_op jit(solution)/shard_map/all_to_all | solution.py:876
  420.5 44.6 %attn_bwd.1 = (bf16[1024,768]{1,0:T(8,128)(2,1)}, f32[4,768,768]{2,1,0:T(8,128)}) custom-call(bf16[1024,768]{1,0:T(8,128)(2,1)} %x_ref.1, bf16[1024,768]{1,0:T(8,128)(2,1)} %get-tuple-element.39.h_ref, bf16[1024,768]{1,0:T(8,128)(2,1)} %dy_ref.3, bf16[1024,768]{1,0:T(8,128)(2,1)} %get-tuple-element.40.q_ref, bf16[1024,768]{1,0:T(8,128)(2,1)} %get-tuple-element.41.k_ref, ...), custom_call_target="tpu_custom_call" | custom-call | flops 15703474176 | bytes 31457280 | tf_op jit(solution)/shard_map/attn_bwd/pallas_call | solution.py:630
  465.1 173.6 %group_sum.1.sum_ref = f32[3072,768]{1,0:T(8,128)} custom-call(f32[3072,768]{1,0:T(8,128)} %bitcast.41), custom_call_target="tpu_custom_call" | custom-call | flops 99999997952 | bytes 18874368 | tf_op jit(solution)/shard_map/group_sum/pallas_call | solution.py:847
  638.7 12.7 %combine.1 = (bf16[1024,768]{1,0:T(8,128)(2,1)}, f32[768,768]{1,0:T(8,128)}, f32[768,768]{1,0:T(8,128)}, f32[768,768]{1,0:T(8,128)}, f32[768,768]{1,0:T(8,128)}) custom-call(bf16[1024,768]{1,0:T(8,128)(2,1)} %get-tuple-element.36.h_ref, bf16[3072,768]{1,0:T(8,128)(2,1)} %bitcast.11.back_ref, s32[1024,1]{1,0:T(8,128)} %copy.35.pos_ref, ...), custom_call_target="tpu_custom_call" | custom-call | flops 1610612736 | bytes 4718592 | tf_op jit(solution)/shard_map/combine/pallas_call | solution.py:665
  (16 shorter events, 1.7 us)
Async XLA Ops:
  193.5 109.6 %all-to-all-start = ((bf16[8,384,768]{2,1,0:T(8,128)(2,1)}), bf16[8,384,768]{2,1,0:T(8,128)(2,1)}, u32[]{:S(2)}, u32[]{:S(2)}) async-start(bf16[8,384,768]{2,1,0:T(8,128)(2,1)} %bitcast.24), calls=%async_computation | async-start | bytes 9437184 | tf_op jit(solution)/shard_map/all_to_all | solution.py:876
  303.1 4.8 copy-start
  303.1 5.6 copy-start.2
  303.1 6.7 %copy-start.1 = (s32[1,1024]{1,0:T(1,128)S(1)}, s32[1,1024]{1,0:T(1,128)}, u32[]{:S(2)}) copy-start(s32[1,1024]{1,0:T(1,128)} %get-tuple-element.47) | copy-start | bytes 12292
  303.1 109.7 %all-to-all-start.2 = ((bf16[8,384,768]{2,1,0:T(8,128)(2,1)}), bf16[8,384,768]{2,1,0:T(8,128)(2,1)}, u32[]{:S(2)}, u32[]{:S(2)}) async-start(bf16[8,384,768]{2,1,0:T(8,128)(2,1)} %bitcast.23), calls=%async_computation.2 | async-start | bytes 9437184 | tf_op jit(solution)/shard_map/all_to_all | solution.py:876
  412.8 225.9 %all-to-all-start.1 = ((bf16[8,384,768]{2,1,0:T(8,128)(2,1)}), bf16[8,384,768]{2,1,0:T(8,128)(2,1)}, u32[]{:S(2)}, u32[]{:S(2)}) async-start(bf16[8,384,768]{2,1,0:T(8,128)(2,1)} %bitcast.25), calls=%async_computation.1 | async-start | bytes 9437184 | tf_op jit(solution)/shard_map/all_to_all | solution.py:876
